TPU v7x, 32 devices: a whole 2x2x4 slice. The times are simulated.
32 devices in a mesh: occ: 4 (over z), vir: 4 (over y, x), ka: 2 (over core).
Axes of the slice: x: 2, y: 2, z: 4, core: 2. Of those that a mesh axis runs over, the one named last changes fastest.
Arguments:
- lambda_amps: bfloat16 [2, 16, 1024, 1024], P(None, 'occ', 'vir', 'ka'), may hold values from -0.25 to 0.25
- screened_ints: bfloat16 [16, 1024, 1024], P(('occ', 'vir'), 'ka'), may hold values from -6 to 6
- half_ints: bfloat16 [16, 1024, 128], P(('occ', 'vir'), 'ka'), may hold values from -0.5 to 0.5
- singles: bfloat16 [128, 1024], P(None, 'vir'), may hold values from -6 to 6
- block_mask: int32 [16, 8, 8], P('occ', 'ka'), may hold values from 0 to 1, as said below
Outputs:
- residual_part: bfloat16 [2, 16, 1024, 1024], P('ka', 'occ', 'vir')
Inputs may be any that keep to these rules, and one draw needn't show every extreme that they name: `block_mask`: for each j and each of the 2 equal ranges of e blocks, between 1 and 16 of its 32 blocks are 1; some (j, range) has exactly 16.
All inputs are finite; a program needn't handle non-finite values.
Results may differ from a plain program's by a relative error of at most 0.0058.
Values may be sent and summed in bfloat16 or wider, within the bound.
A program may use at most 128 MiB of HBM per device.

v0:
```python
import functools

import jax
import jax.numpy as jnp
from jax import lax
from jax.experimental import pallas as pl
from jax.experimental.pallas import tpu as pltpu
from jax.sharding import PartitionSpec as P

TILE = 128
CAP = 16
SIDES = 2
CHUNKS = 2


def peers_of(v, n, grid):
    if grid:
        y, x = v // 2, v % 2
        ids = [v, y * 2 + (1 - x), (1 - y) * 2 + x, (1 - y) * 2 + (1 - x)]
        return ids, ids
    return [(v + k) % n for k in range(n)], [(v + n - k) % n for k in range(n)]


def kernel(n, lam, x, y, t, mask, out, lam_v, x_v, y_v, dressed, dense, own, give, take, following,
           in_sem, t_send, t_recv, b_send, b_recv, f_send, p_send, p_recv, *bufs):
    t_v, gath = bufs[:n], bufs[n:]
    grid = n == 4
    v, c = lax.axis_index("vir"), lax.axis_index("ka")
    dst, src = peers_of(v, n, grid)
    partner = 1 - c
    half = x_v.shape[0]
    width = t_v[0].shape[1]
    cols = width // TILE
    row_blocks = half // TILE
    col_blocks = x_v.shape[1] // TILE
    blocks = row_blocks * col_blocks
    per = CAP // CHUNKS

    loads = [
        pltpu.make_async_copy(t, t_v[0], in_sem.at[0]),
        pltpu.make_async_copy(y.at[0], y_v, in_sem.at[1]),
        pltpu.make_async_copy(x.at[0], x_v, in_sem.at[2]),
        pltpu.make_async_copy(lam, lam_v, in_sem.at[3]),
    ]
    for load in loads:
        load.start()

    barrier = pltpu.get_barrier_semaphore()
    for k in range(1, n):
        pl.semaphore_signal(barrier, inc=1, device_id={"vir": dst[k]}, device_id_type=pl.DeviceIdType.MESH)
    pl.semaphore_signal(barrier, inc=1, device_id={"ka": partner}, device_id_type=pl.DeviceIdType.MESH)
    loads[0].wait()
    pl.semaphore_wait(barrier, n)

    def remote(source, target, send, recv, where):
        return pltpu.make_async_remote_copy(
            src_ref=source, dst_ref=target, send_sem=send, recv_sem=recv,
            device_id=where, device_id_type=pl.DeviceIdType.MESH)

    t_copies = [None] + [
        remote(t_v[0], t_v[k], t_send.at[k], t_recv.at[k], {"vir": dst[k]})
        for k in range(1, n)]
    for copy in reversed(t_copies[1:]):
        copy.start()

    following[blocks] = blocks - 1
    later = jnp.int32(blocks - 1)
    for p in reversed(range(blocks)):
        later = jnp.where(mask[v, p // col_blocks, p % col_blocks] != 0, p, later)
        following[p] = later

    loads[1].wait()
    loads[2].wait()

    def dress(k):
        start = src[k] * width
        term = jnp.dot(y_v[...], t_v[k][...], preferred_element_type=jnp.float32)
        part = (x_v[:, pl.ds(pl.multiple_of(start, TILE), width)].astype(jnp.float32) - term).astype(jnp.bfloat16)
        for e in range(row_blocks):
            for b in range(cols):
                dressed[e * col_blocks + src[k] * cols + b] = part[e * TILE:(e + 1) * TILE, b * TILE:(b + 1) * TILE]

    dress(0)
    for k in range(1, n):
        t_copies[k].wait_recv()
    for k in range(1, n):
        dress(k)

    def chunk(ref, q):
        return ref.at[pl.ds(q * per, per)]

    def own_copy(k, q):
        return remote(chunk(gath[0], q), chunk(gath[k], q), b_send.at[k, q], b_recv.at[k, q], {"vir": dst[k]})

    def relay_copy(k, q):
        return remote(chunk(gath[k], q), chunk(gath[3], q), f_send.at[q], b_recv.at[3, q], {"vir": dst[3 - k]})

    direct = (1, 2) if grid else tuple(range(1, n))
    relays = [(1, q) for q in range(CHUNKS // 2)] + [(2, q) for q in range(CHUNKS // 2, CHUNKS)]
    place = jnp.int32(-1)
    order = []
    for s in range(CAP):
        place = following[jnp.minimum(place + 1, blocks)]
        order.append(place)
    halves = (list(range(CHUNKS // 2)), list(range(CHUNKS // 2, CHUNKS)))
    for low, high in zip(*halves):
        for q in (low, high):
            for s in range(q * per, (q + 1) * per):
                gath[0][s] = dressed[order[s]]
        if grid:
            own_copy(1, low).start()
            own_copy(2, high).start()
    if grid:
        for low, high in zip(*halves):
            own_copy(1, high).start()
            own_copy(2, low).start()
    else:
        for k in direct:
            for q in range(CHUNKS):
                own_copy(k, q).start()

    side = x_v.shape[1] // SIDES

    def partner_copy(k, h):
        columns = pl.ds(h * side, side)
        return remote(give.at[k, :, columns], take.at[k, :, columns], p_send.at[k, h], p_recv.at[k, h], {"ka": partner})

    def form(k):
        j = src[k]

        def rows(e, count):
            for b in range(col_blocks):
                live = mask[j, e, b]
                block = gath[k][jnp.minimum(count, CAP - 1)]
                dense[pl.ds(pl.multiple_of(e * TILE, TILE), TILE), b * TILE:(b + 1) * TILE] = jnp.where(
                    live != 0, block, jnp.zeros_like(block))
                count = count + live
            return count

        lax.fori_loop(0, row_blocks, rows, jnp.int32(0))
        for h in range(SIDES):
            columns = slice(h * side, (h + 1) * side)
            give[k, :, columns] = jnp.dot(
                lam_v[partner, j], dense[:, columns], preferred_element_type=jnp.float32).astype(jnp.bfloat16)
            partner_copy(k, h).start()
        own[k] = jnp.dot(lam_v[c, j], dense[...], preferred_element_type=jnp.float32)

    def finish(k):
        for h in range(SIDES):
            columns = slice(h * side, (h + 1) * side)
            partner_copy(k, h).wait_recv()
            out[0, src[k], :, columns] = (
                own[k, :, columns] + take[k, :, columns].astype(jnp.float32)).astype(jnp.bfloat16)

    loads[3].wait()
    form(0)
    if grid:
        for k, q in relays:
            own_copy(k, q).wait_recv()
            relay_copy(k, q).start()
        done = set(relays)
    else:
        done = set()
    for k in range(1, n):
        if k == n - 1:
            finish(k - 1)
        for q in range(CHUNKS):
            if (k, q) not in done:
                own_copy(k, q).wait_recv()
        form(k)
        if k < n - 1:
            finish(k - 1)
    finish(n - 1)

    for k in range(1, n):
        t_copies[k].wait_send()
    for k in direct:
        for q in range(CHUNKS):
            own_copy(k, q).wait_send()
    if grid:
        for k, q in relays:
            relay_copy(k, q).wait_send()
    for k in range(n):
        for h in range(SIDES):
            partner_copy(k, h).wait_send()


def body(n, lambda_amps, screened_ints, half_ints, singles, block_mask):
    wide, pairs, rows, half = lambda_amps.shape
    full = screened_ints.shape[2]
    inner, width = singles.shape
    blocks = (half // TILE) * (full // TILE)
    bf16, f32 = jnp.bfloat16, jnp.float32
    dma = pltpu.SemaphoreType.DMA
    anywhere = pl.BlockSpec(memory_space=pl.ANY)
    return pl.pallas_call(
        functools.partial(kernel, n),
        out_shape=pltpu.VMEM((1, pairs, rows, full), bf16),
        in_specs=[anywhere] * 4 + [pl.BlockSpec(memory_space=pltpu.SMEM)],
        out_specs=pl.BlockSpec(memory_space=pltpu.VMEM),
        scratch_shapes=[
            pltpu.VMEM(lambda_amps.shape, bf16),
            pltpu.VMEM((half, full), bf16),
            pltpu.VMEM((half, inner), bf16),
            pltpu.VMEM((blocks, TILE, TILE), bf16),
            pltpu.VMEM((half, full), bf16),
            pltpu.VMEM((n, rows, full), f32),
            pltpu.VMEM((n, rows, full), bf16),
            pltpu.VMEM((n, rows, full), bf16),
            pltpu.SMEM((blocks + 1,), jnp.int32),
            dma((4,)), dma((n,)), dma((n,)), dma((n, CHUNKS)), dma((n, CHUNKS)), dma((CHUNKS,)),
            dma((n, SIDES)), dma((n, SIDES)),
        ] + [pltpu.VMEM((inner, width), bf16)] * n + [pltpu.VMEM((CAP, TILE, TILE), bf16)] * n,
        compiler_params=pltpu.CompilerParams(
            collective_id=0, has_side_effects=True, vmem_limit_bytes=56 * 1024 * 1024),
    )(lambda_amps, screened_ints, half_ints, singles, block_mask)


def solution(mesh):
    return jax.shard_map(
        functools.partial(body, mesh.shape["vir"]),
        mesh=mesh,
        in_specs=(
            P(None, "occ", "vir", "ka"),
            P(("occ", "vir"), "ka", None),
            P(("occ", "vir"), "ka", None),
            P(None, "vir"),
            P("occ", "ka", None),
        ),
        out_specs=P("ka", "occ", "vir", None),
        check_vma=False,
    )
```

profile of v0, /device:TPU:0, one launch (start us, length us, event | category | flops | bytes accessed | tf_op | source)
XLA Modules:
  0.0 31.8 jit_solution(17494348974973422500)
XLA Ops:
  0.0 30.5 %shard_map.55 = bf16[1,4,256,1024]{3,2,1,0:T(8,128)(2,1)S(1)} custom-call(bf16[2,4,256,512]{3,2,1,0:T(8,128)(2,1)} %lam.1, bf16[1,512,1024]{2,1,0:T(8,128)(2,1)} %x.1, bf16[1,512,128]{2,1,0:T(8,128)(2,1)} %y.1, bf16[128,256]{1,0:T(8,128)(2,1)} %t.1, s32[4,4,8]{2,1,0:T(4,128)} %mask.1), custom_call_target="tpu_custom_call" | custom-call | tf_op jit(solution)/shard_map/pallas_call | solution.py:196
  30.5 1.3 %copy.7 = bf16[1,4,256,1024]{3,2,1,0:T(8,128)(2,1)} copy(bf16[1,4,256,1024]{3,2,1,0:T(8,128)(2,1)S(1)} %shard_map.55) | data formatting | bytes 4194304
where the time goes:
time: 32 us; the launch traced here: 31.8 us
  Pallas kernels  30.5 us (95%)
  local copies, waits for them, and re-layouts  1.32 us (4%)
    pallas_call x1, Pallas kernels, body(): pl.pallas_call(functools.partial(kernel, n), out_shape=pltpu.VMEM((1, pai...  30.5 us
    unnamed x1, local copies, waits for them, and re-layouts  1.32 us

commit v1 on v0

v1 whole, which is shorter than its diff:
```python
import functools

import jax
import jax.numpy as jnp
from jax import lax
from jax.experimental import pallas as pl
from jax.experimental.pallas import tpu as pltpu
from jax.sharding import PartitionSpec as P

TILE = 128
CAP = 16
PER = 2
CHUNKS = CAP // PER


def peers_of(v, n, grid):
    if grid:
        y, x = v // 2, v % 2
        ids = [v, y * 2 + (1 - x), (1 - y) * 2 + x, (1 - y) * 2 + (1 - x)]
        return ids, ids
    return [(v + k) % n for k in range(n)], [(v + n - k) % n for k in range(n)]


def kernel(n, lam, x, y, t, mask, mask_any, out, lam_m, lam_t, x_v, y_v, dressed, dense_m, dense_t, acc, other,
           in_sem, t_send, t_recv, td_send, td_recv, b_send, b_recv, f_send, d_send, d_recv, l_send, l_recv, *bufs):
    t_v, mine, theirs = bufs[:n], bufs[n:2 * n], bufs[2 * n:]
    grid = n == 4
    v, c = lax.axis_index("vir"), lax.axis_index("ka")
    dst, src = peers_of(v, n, grid)
    partner = 1 - c
    half = x_v.shape[0]
    inner, width = t_v[0].shape
    cols = width // TILE
    row_blocks = half // TILE
    col_blocks = x_v.shape[1] // TILE
    part = inner // 2

    loads = [
        pltpu.make_async_copy(t, t_v[0], in_sem.at[0]),
        pltpu.make_async_copy(y.at[0], y_v, in_sem.at[1]),
        pltpu.make_async_copy(x.at[0], x_v, in_sem.at[2]),
        pltpu.make_async_copy(lam.at[c], lam_m, in_sem.at[3]),
    ]
    for load in loads:
        load.start()

    barrier = pltpu.get_barrier_semaphore()
    for k in range(1, n):
        pl.semaphore_signal(barrier, inc=1, device_id={"vir": dst[k]}, device_id_type=pl.DeviceIdType.MESH)
    pl.semaphore_signal(barrier, inc=1, device_id={"ka": partner}, device_id_type=pl.DeviceIdType.MESH)
    loads[0].wait()
    pl.semaphore_wait(barrier, n)

    def remote(source, target, send, recv, where):
        return pltpu.make_async_remote_copy(
            src_ref=source, dst_ref=target, send_sem=send, recv_sem=recv,
            device_id=where, device_id_type=pl.DeviceIdType.MESH)

    def rows_of(ref):
        return ref.at[pl.ds(pl.multiple_of(c * part, part), part)]

    t_copies = [None] + [
        remote(rows_of(t_v[0]), rows_of(t_v[k]), t_send.at[k], t_recv.at[k], {"vir": dst[k]})
        for k in range(1, n)]
    t_swaps = [None] + [
        remote(rows_of(t_v[k]), rows_of(t_v[k]), td_send.at[k], td_recv.at[k], {"ka": partner})
        for k in range(1, n)]
    for copy in reversed(t_copies[1:]):
        copy.start()
    mask_swap = remote(mask_any, other, l_send.at[0], l_recv.at[0], {"ka": partner})
    mask_swap.start()

    zero = jnp.zeros((TILE, TILE), jnp.bfloat16)
    for k in range(n):
        mine[k][CAP] = zero
        theirs[k][CAP] = zero

    blocks = row_blocks * col_blocks
    order = [jnp.int32(0)] * CAP
    count = jnp.int32(0)
    for p in range(blocks):
        live = mask[v, p // col_blocks, p % col_blocks]
        order = [jnp.where((live != 0) & (count == s), p, order[s]) for s in range(CAP)]
        count = count + live

    loads[1].wait()
    loads[2].wait()

    def dress(k):
        start = src[k] * width
        term = jnp.dot(y_v[...], t_v[k][...], preferred_element_type=jnp.float32)
        value = (x_v[:, pl.ds(pl.multiple_of(start, TILE), width)].astype(jnp.float32) - term).astype(jnp.bfloat16)
        for e in range(row_blocks):
            for b in range(cols):
                dressed[e * col_blocks + src[k] * cols + b] = value[e * TILE:(e + 1) * TILE, b * TILE:(b + 1) * TILE]

    dress(0)
    for k in range(1, n):
        t_copies[k].wait_recv()
        t_swaps[k].start()
    for k in range(1, n):
        t_swaps[k].wait_recv()
        dress(k)

    def chunk(ref, q):
        return ref.at[pl.ds(q * PER, PER)]

    def own_copy(k, q):
        return remote(chunk(mine[0], q), chunk(mine[k], q), b_send.at[k, q], b_recv.at[k, q], {"vir": dst[k]})

    def relay_copy(k, q):
        return remote(chunk(mine[k], q), chunk(mine[3], q), f_send.at[q], b_recv.at[3, q], {"vir": dst[3 - k]})

    def swap(k, q):
        return remote(chunk(mine[k], q), chunk(theirs[k], q), d_send.at[k, q], d_recv.at[k, q], {"ka": partner})

    low, high = list(range(CHUNKS // 2)), list(range(CHUNKS // 2, CHUNKS))
    direct = (1, 2) if grid else tuple(range(1, n))
    paths = {k: (high + low if grid and k == 2 else low + high) for k in range(1, n)}
    relays = [(1, q) for q in low] + [(2, q) for q in high] if grid else []

    for pair in zip(low, high):
        for q in pair:
            for s in range(q * PER, (q + 1) * PER):
                mine[0][s] = dressed[order[s]]
            if not grid:
                for k in direct:
                    own_copy(k, q).start()
        if grid:
            own_copy(1, pair[0]).start()
            own_copy(2, pair[1]).start()
    if grid:
        for pair in zip(low, high):
            own_copy(1, pair[1]).start()
            own_copy(2, pair[0]).start()
    for q in range(CHUNKS):
        swap(0, q).start()
    lam_swap = remote(lam.at[partner], lam_t, l_send.at[1], l_recv.at[1], {"ka": partner})
    lam_swap.start()
    mask_swap.wait_recv()

    def fill(dense, gathered, live_of, j):
        count = jnp.int32(0)
        for e in range(row_blocks):
            for b in range(col_blocks):
                live = live_of[j, e, b]
                dense[e * TILE:(e + 1) * TILE, b * TILE:(b + 1) * TILE] = gathered[jnp.where(live != 0, count, CAP)]
                count = count + live

    def first(k):
        fill(dense_m, mine[k], mask, src[k])
        acc[...] = jnp.dot(lam_m[src[k]], dense_m[...], preferred_element_type=jnp.float32)

    def second(k):
        for q in range(CHUNKS):
            swap(k, q).wait_recv()
        fill(dense_t, theirs[k], other, src[k])
        out[0, src[k]] = (acc[...] + jnp.dot(
            lam_t[src[k]], dense_t[...], preferred_element_type=jnp.float32)).astype(jnp.bfloat16)

    def arrive(k, q):
        own_copy(k, q).wait_recv()
        if (k, q) in relays:
            relay_copy(k, q).start()
        swap(k, q).start()

    loads[3].wait()
    first(0)
    lam_swap.wait_recv()
    second(0)
    if grid:
        for i in range(CHUNKS):
            for k in direct:
                arrive(k, paths[k][i])
        first(1)
        second(1)
        arrive(3, low[0])
        arrive(3, high[0])
        first(2)
        second(2)
        for pair in zip(low[1:], high[1:]):
            arrive(3, pair[0])
            arrive(3, pair[1])
        first(3)
        second(3)
    else:
        for k in direct:
            for q in range(CHUNKS):
                arrive(k, q)
            first(k)
            second(k)

    for k in range(1, n):
        t_copies[k].wait_send()
        t_swaps[k].wait_send()
    mask_swap.wait_send()
    lam_swap.wait_send()
    for k in direct:
        for q in range(CHUNKS):
            own_copy(k, q).wait_send()
    for k, q in relays:
        relay_copy(k, q).wait_send()
    for k in range(n):
        for q in range(CHUNKS):
            swap(k, q).wait_send()


def body(n, lambda_amps, screened_ints, half_ints, singles, block_mask):
    wide, pairs, rows, half = lambda_amps.shape
    full = screened_ints.shape[2]
    inner, width = singles.shape
    blocks = (half // TILE) * (full // TILE)
    bf16, f32 = jnp.bfloat16, jnp.float32
    dma = pltpu.SemaphoreType.DMA
    anywhere = pl.BlockSpec(memory_space=pl.ANY)
    return pl.pallas_call(
        functools.partial(kernel, n),
        out_shape=pltpu.VMEM((1, pairs, rows, full), bf16),
        in_specs=[anywhere] * 4 + [pl.BlockSpec(memory_space=pltpu.SMEM), anywhere],
        out_specs=pl.BlockSpec(memory_space=pltpu.VMEM),
        scratch_shapes=[
            pltpu.VMEM((pairs, rows, half), bf16),
            pltpu.VMEM((pairs, rows, half), bf16),
            pltpu.VMEM((half, full), bf16),
            pltpu.VMEM((half, inner), bf16),
            pltpu.VMEM((blocks, TILE, TILE), bf16),
            pltpu.VMEM((half, full), bf16),
            pltpu.VMEM((half, full), bf16),
            pltpu.VMEM((rows, full), f32),
            pltpu.SMEM(block_mask.shape, jnp.int32),
            dma((4,)), dma((n,)), dma((n,)), dma((n,)), dma((n,)), dma((n, CHUNKS)), dma((n, CHUNKS)),
            dma((CHUNKS,)), dma((n, CHUNKS)), dma((n, CHUNKS)), dma((2,)), dma((2,)),
        ] + [pltpu.VMEM((inner, width), bf16)] * n + [pltpu.VMEM((CAP + 1, TILE, TILE), bf16)] * (2 * n),
        compiler_params=pltpu.CompilerParams(
            collective_id=0, has_side_effects=True, vmem_limit_bytes=56 * 1024 * 1024),
    )(lambda_amps, screened_ints, half_ints, singles, block_mask, block_mask)


def solution(mesh):
    return jax.shard_map(
        functools.partial(body, mesh.shape["vir"]),
        mesh=mesh,
        in_specs=(
            P(None, "occ", "vir", "ka"),
            P(("occ", "vir"), "ka", None),
            P(("occ", "vir"), "ka", None),
            P(None, "vir"),
            P("occ", "ka", None),
        ),
        out_specs=P("ka", "occ", "vir", None),
        check_vma=False,
    )
```

time: 32 us -> 32.5 us (1.016)
  Pallas kernels: 30.5 us -> 31 us
    pallas_call x1, Pallas kernels: 30.5 us -> 31 us  [body(): pl.pallas_call(functools.partial(kernel, n), out_shape=pltpu.VMEM((1, pai...]
where the time goes in v1:
time: 32.5 us; the launch traced here: 32.3 us
  Pallas kernels  31 us (95%)
  local copies, waits for them, and re-layouts  1.32 us (4%)
    pallas_call x1, Pallas kernels, body(): pl.pallas_call(functools.partial(kernel, n), out_shape=pltpu.VMEM((1, pai...  31 us
    unnamed x1, local copies, waits for them, and re-layouts  1.32 us

profile of v1, /device:TPU:0, one launch (start us, length us, event | category | flops | bytes accessed | tf_op | source)
XLA Modules:
  0.0 32.3 jit_solution(16880986346420497639)
XLA Ops:
  0.0 31.0 %shard_map.55 = bf16[1,4,256,1024]{3,2,1,0:T(8,128)(2,1)S(1)} custom-call(bf16[2,4,256,512]{3,2,1,0:T(8,128)(2,1)} %lam.1, bf16[1,512,1024]{2,1,0:T(8,128)(2,1)} %x.1, bf16[1,512,128]{2,1,0:T(8,128)(2,1)} %y.1, bf16[128,256]{1,0:T(8,128)(2,1)} %t.1, s32[4,4,8]{2,1,0:T(4,128)} %mask_any.1, s32[4,4,8]{2,1,0:T(4,128)} %mask_any.1), custom_call_target="tpu_custom_call" | custom-call | tf_op jit(solution)/shard_map/pallas_call | solution.py:216
  31.0 1.3 %copy.7 = bf16[1,4,256,1024]{3,2,1,0:T(8,128)(2,1)} copy(bf16[1,4,256,1024]{3,2,1,0:T(8,128)(2,1)S(1)} %shard_map.55) | data formatting | bytes 4194304

commit v2 on v1

v2 whole, which is shorter than its diff:
```python
import functools

import jax
import jax.numpy as jnp
from jax import lax
from jax.experimental import pallas as pl
from jax.experimental.pallas import tpu as pltpu
from jax.sharding import PartitionSpec as P

TILE = 128
CAP = 16
MESH = pl.DeviceIdType.MESH


def remote(source, target, send, recv, where):
    return pltpu.make_async_remote_copy(
        src_ref=source, dst_ref=target, send_sem=send, recv_sem=recv, device_id=where, device_id_type=MESH)


def enter(places):
    barrier = pltpu.get_barrier_semaphore()
    for place in places:
        pl.semaphore_signal(barrier, inc=1, device_id=place, device_id_type=MESH)
    return barrier


def top_row(live_of, j, row_blocks, col_blocks):
    best, most = jnp.int32(0), jnp.int32(-1)
    for e in range(row_blocks):
        total = live_of[j, e, 0]
        for b in range(1, col_blocks):
            total = total + live_of[j, e, b]
        best = jnp.where(total > most, e, best)
        most = jnp.maximum(total, most)
    return best


def raw_columns(live_of, j, row, raw, col_blocks):
    found = [jnp.int32(0)] * raw
    rank = jnp.int32(0)
    for b in range(col_blocks):
        live = live_of[j, row, b]
        found = [jnp.where((live != 0) & (rank == s), b, found[s]) for s in range(raw)]
        rank = rank + live
    return found


def slots_of(live_of, j, row, raw, late, row_blocks, col_blocks, cols):
    early_next, late_next = jnp.int32(raw), jnp.int32(CAP - 1)
    is_late = [late == g for g in range(col_blocks // cols)]
    slots = []
    for e in range(row_blocks):
        room = jnp.where(row == e, raw, 0)
        rank = jnp.int32(0)
        for b in range(col_blocks):
            live = live_of[j, e, b]
            is_raw = rank < room
            behind = is_late[b // cols]
            slot = jnp.where(is_raw, rank, jnp.where(behind, late_next, early_next))
            slots.append(jnp.where(live != 0, slot, CAP))
            step = jnp.where(is_raw, 0, live)
            late_next = late_next - jnp.where(behind, step, 0)
            early_next = early_next + jnp.where(behind, 0, step)
            rank = rank + live
    return slots


def grid_kernel(lam, x, y, t, mask_any, out, lam_m, lam_t, x_v, y_v, t_v, dressed, dense_m, dense_t, acc, mask, other,
                in_sem, x_sem, t_send, t_recv, td_send, td_recv, b_send, b_recv, f_send, d_send, d_recv, l_send, l_recv,
                *bufs):
    n = 4
    mine, theirs, raw_m, raw_t = bufs[:n], bufs[n:2 * n], bufs[2 * n:3 * n], bufs[3 * n:]
    v, c = lax.axis_index("vir"), lax.axis_index("ka")
    row, col = v // 2, v % 2
    ids = [v, row * 2 + (1 - col), (1 - row) * 2 + col, (1 - row) * 2 + (1 - col)]
    partner = 1 - c
    row_blocks, col_blocks = y_v.shape[0], t_v.shape[0]
    inner = t_v.shape[1]
    cols = col_blocks // n
    part = inner // 2
    raw = CAP // row_blocks
    late = row_blocks * cols
    first = CAP - raw - late
    f32, bf16 = jnp.float32, jnp.bfloat16

    def block(e, b):
        return x.at[0, pl.ds(e * TILE, TILE), pl.ds(b * TILE, TILE)]

    mask_load = pltpu.make_async_copy(mask_any, mask, in_sem.at[0])
    t_loads = [pltpu.make_async_copy(
        t.at[:, pl.ds(i * TILE, TILE)], t_v.at[v * cols + i], in_sem.at[1 + i]) for i in range(cols)]
    y_loads = [pltpu.make_async_copy(
        y.at[0, pl.ds(e * TILE, TILE)], y_v.at[e], in_sem.at[1 + cols + e]) for e in range(row_blocks)]
    x_loads = [pltpu.make_async_copy(
        block(p // col_blocks, p % col_blocks), x_v.at[p], x_sem.at[p]) for p in range(row_blocks * col_blocks)]
    lam_load = pltpu.make_async_copy(lam.at[c], lam_m, in_sem.at[1 + cols + row_blocks])
    mask_load.start()
    for load in t_loads + y_loads + x_loads:
        load.start()
    lam_load.start()
    to_x, to_y, to_core = {"vir": ids[1]}, {"vir": ids[2]}, {"ka": partner}
    near = [None, to_x, to_y]
    barrier = enter([to_x, to_y, to_core])

    zero = jnp.zeros((TILE, TILE), bf16)
    for k in range(n):
        mine[k][CAP] = zero
        theirs[k][CAP] = zero

    mask_load.wait()
    lead = top_row(mask, v, row_blocks, col_blocks)
    lead_columns = raw_columns(mask, v, lead, raw, col_blocks)
    for load in t_loads:
        load.wait()
    pl.semaphore_wait(barrier, 3)

    def t_part(k):
        return t_v.at[pl.ds(ids[k] * cols, cols), pl.ds(pl.multiple_of(c * part, part), part)]

    t_copies = [None] + [remote(t_part(0), t_part(0), t_send.at[k], t_recv.at[k], near[k]) for k in (1, 2)]
    t_relay = remote(t_part(1), t_part(1), t_send.at[3], t_recv.at[3], to_y)
    t_swaps = [None] + [remote(t_part(k), t_part(k), td_send.at[k], td_recv.at[k], to_core) for k in (1, 2, 3)]
    for k in (1, 2):
        t_copies[k].start()
    mask_swap = remote(mask_any, other, l_send.at[0], l_recv.at[0], to_core)
    mask_swap.start()

    for load in y_loads + x_loads:
        load.wait()
    for s in range(raw):
        raw_m[0][s] = x_v[lead * col_blocks + lead_columns[s]]
    raw_m[0][raw] = y_v[lead]

    spans = [(0, raw // 2), (raw // 2, raw + 1)]
    at = raw
    for size in [first // 2] * 2 + [late // 4] * 4:
        spans.append((at, at + size))
        at += size
    chunks = len(spans)
    low, high = (0, 2, 4, 5), (1, 3, 6, 7)
    paths = [None, (0, 1, 2, 3, 4, 5, 6, 7), (1, 0, 3, 2, 6, 7, 4, 5)]

    def chunk(raws, gathered, k, q):
        start, stop = spans[q]
        return (raws if q < 2 else gathered)[k].at[pl.ds(start, stop - start)]

    def here(k, q):
        return chunk(raw_m, mine, k, q)

    def own_copy(k, q):
        return remote(here(0, q), here(k, q), b_send.at[k, q], b_recv.at[k, q], near[k])

    def relay_copy(k, q):
        return remote(here(k, q), here(3, q), f_send.at[q], b_recv.at[3, q], near[3 - k])

    def swap(k, q):
        if k == 0 and q == 0:
            return remote(mine[0].at[pl.ds(0, raw)], theirs[0].at[pl.ds(0, raw)], d_send.at[0, 0], d_recv.at[0, 0], to_core)
        return remote(here(k, q), chunk(raw_t, theirs, k, q), d_send.at[k, q], d_recv.at[k, q], to_core)

    relays = [(1, q) for q in low] + [(2, q) for q in high]

    own_copy(1, 0).start()
    own_copy(2, 1).start()
    own_copy(1, 1).start()

    def dress(k):
        for i in range(cols):
            b = ids[k] * cols + i
            columns = t_v[b]
            for e in range(row_blocks):
                term = jnp.dot(y_v[e], columns, preferred_element_type=f32)
                dressed[e * col_blocks + b] = (x_v[e * col_blocks + b].astype(f32) - term).astype(bf16)

    slots = slots_of(mask, v, lead, raw, n - 1 - v, row_blocks, col_blocks, cols)
    order = []
    for s in range(raw, CAP):
        place = jnp.int32(0)
        for p, slot in enumerate(slots):
            place = jnp.where(slot == s, p, place)
        order.append(place)

    dress(0)
    t_copies[1].wait_recv()
    t_relay.start()
    own_copy(2, 0).start()
    t_swaps[1].start()
    t_copies[2].wait_recv()
    t_swaps[2].start()
    for k in (1, 2):
        t_swaps[k].wait_recv()
        dress(k)

    def pack(q):
        for s in range(*spans[q]):
            mine[0][s] = dressed[order[s - raw]]

    pack(2)
    pack(3)
    for i in (2, 3):
        for k in (1, 2):
            own_copy(k, paths[k][i]).start()
    t_relay.wait_recv()
    t_swaps[3].start()
    t_swaps[3].wait_recv()
    dress(3)
    for i in range(4, chunks):
        if i < 6:
            for k in (1, 2):
                pack(paths[k][i])
        for k in (1, 2):
            own_copy(k, paths[k][i]).start()
    for s in range(raw):
        mine[0][s] = dressed[lead * col_blocks + lead_columns[s]]
    swaps_of = [[0] + list(range(2, chunks))] + [list(range(chunks))] * 3
    for q in swaps_of[0]:
        swap(0, q).start()
    lam_swap = remote(lam.at[partner], lam_t, l_send.at[1], l_recv.at[1], to_core)
    lam_swap.start()
    mask_swap.wait_recv()

    def mend(k, raws, gathered, live_of):
        best = top_row(live_of, ids[k], row_blocks, col_blocks)
        places = raw_columns(live_of, ids[k], best, raw, col_blocks)
        rows = raws[k][raw]
        for s in range(raw):
            term = jnp.dot(rows, t_v[places[s]], preferred_element_type=f32)
            gathered[k][s] = (raws[k][s].astype(f32) - term).astype(bf16)

    def fill(dense, gathered, live_of, k):
        j = ids[k]
        best = top_row(live_of, j, row_blocks, col_blocks)
        slots = slots_of(live_of, j, best, raw, n - 1 - j, row_blocks, col_blocks, cols)
        for p, slot in enumerate(slots):
            e, b = p // col_blocks, p % col_blocks
            dense[e * TILE:(e + 1) * TILE, b * TILE:(b + 1) * TILE] = gathered[k][slot]

    def own_half(k):
        fill(dense_m, mine, mask, k)
        acc[...] = jnp.dot(lam_m[ids[k]], dense_m[...], preferred_element_type=f32)

    def other_half(k):
        for q in swaps_of[k]:
            if k == 0 or q >= 2:
                swap(k, q).wait_recv()
        fill(dense_t, theirs, other, k)
        out[0, ids[k]] = (acc[...] + jnp.dot(
            lam_t[ids[k]], dense_t[...], preferred_element_type=f32)).astype(bf16)

    def arrive(k, q):
        own_copy(1, q).wait_recv() if k == 1 else own_copy(2, q).wait_recv() if k == 2 else relay_copy(1, q).wait_recv()
        if (k, q) in relays:
            relay_copy(k, q).start()
        swap(k, q).start()

    def mend_both(k):
        mend(k, raw_m, mine, mask)
        for q in (0, 1):
            swap(k, q).wait_recv()
        mend(k, raw_t, theirs, other)

    for i in (0, 1):
        for k in (1, 2):
            arrive(k, paths[k][i])
    mend_both(1)
    mend_both(2)
    for i in (2, 3):
        for k in (1, 2):
            arrive(k, paths[k][i])
    lam_load.wait()
    lam_swap.wait_recv()
    own_half(0)
    other_half(0)
    for i in range(4, chunks):
        for k in (1, 2):
            arrive(k, paths[k][i])
    own_half(1)
    other_half(1)
    arrive(3, 0)
    arrive(3, 1)
    mend_both(3)
    own_half(2)
    other_half(2)
    for pair in zip(low[1:], high[1:]):
        for q in pair:
            arrive(3, q)
    own_half(3)
    other_half(3)

    for k in (1, 2):
        t_copies[k].wait_send()
        for q in range(chunks):
            own_copy(k, q).wait_send()
    t_relay.wait_send()
    for k in (1, 2, 3):
        t_swaps[k].wait_send()
    mask_swap.wait_send()
    lam_swap.wait_send()
    for k, q in relays:
        relay_copy(k, q).wait_send()
    for k in range(n):
        for q in swaps_of[k]:
            swap(k, q).wait_send()


def ring_kernel(n, lam, x, y, t, mask_any, out, lam_m, lam_t, x_v, y_v, t_v, dressed, dense_m, dense_t, acc, mask, other,
                in_sem, t_send, t_recv, b_send, b_recv, d_send, d_recv, l_send, l_recv, *bufs):
    mine, theirs = bufs[:n], bufs[n:]
    v, c = lax.axis_index("vir"), lax.axis_index("ka")
    dst, src = [(v + k) % n for k in range(n)], [(v + n - k) % n for k in range(n)]
    half, full = x_v.shape
    width = t_v.shape[2]
    row_blocks, col_blocks = half // TILE, full // TILE
    f32, bf16 = jnp.float32, jnp.bfloat16
    loads = [pltpu.make_async_copy(source, target, in_sem.at[i]) for i, (source, target) in enumerate(
        [(mask_any, mask), (t, t_v.at[v]), (y.at[0], y_v), (x.at[0], x_v), (lam.at[c], lam_m)])]
    for load in loads:
        load.start()
    to_core = {"ka": 1 - c}
    barrier = enter([{"vir": dst[k]} for k in range(1, n)] + [to_core])
    for load in loads:
        load.wait()
    pl.semaphore_wait(barrier, n)

    t_copies = [remote(t_v.at[v], t_v.at[v], t_send.at[k], t_recv.at[k], {"vir": dst[k]}) for k in range(1, n)]
    arrivals = [remote(t_v.at[v], t_v.at[src[k]], t_send.at[k], t_recv.at[k], {"vir": dst[k]}) for k in range(1, n)]
    for copy in t_copies:
        copy.start()
    mask_swap = remote(mask_any, other, l_send.at[0], l_recv.at[0], to_core)
    lam_swap = remote(lam.at[1 - c], lam_t, l_send.at[1], l_recv.at[1], to_core)
    mask_swap.start()
    lam_swap.start()

    zero = jnp.zeros((TILE, TILE), bf16)
    for k in range(n):
        mine[k][CAP] = zero
        theirs[k][CAP] = zero
    order = [jnp.int32(0)] * CAP
    count = jnp.int32(0)
    for p in range(row_blocks * col_blocks):
        live = mask[v, p // col_blocks, p % col_blocks]
        order = [jnp.where((live != 0) & (count == s), p, order[s]) for s in range(CAP)]
        count = count + live

    for copy in arrivals:
        copy.wait_recv()
    for b in range(col_blocks):
        if width >= TILE:
            owner, offset = b * TILE // width, b * TILE % width
            columns = t_v[owner][:, offset:offset + TILE]
        else:
            group = TILE // width
            columns = jnp.concatenate([t_v[b * group + i] for i in range(group)], axis=1)
        term = jnp.dot(y_v[...], columns, preferred_element_type=f32)
        value = (x_v[:, b * TILE:(b + 1) * TILE].astype(f32) - term).astype(bf16)
        for e in range(row_blocks):
            dressed[e * col_blocks + b] = value[e * TILE:(e + 1) * TILE]
    for s in range(CAP):
        mine[0][s] = dressed[order[s]]

    def live_part(ref):
        return ref.at[pl.ds(0, CAP)]

    copies = [None] + [
        remote(live_part(mine[0]), live_part(mine[k]), b_send.at[k], b_recv.at[k], {"vir": dst[k]}) for k in range(1, n)]
    swaps = [remote(live_part(mine[k]), live_part(theirs[k]), d_send.at[k], d_recv.at[k], to_core) for k in range(n)]
    for copy in copies[1:]:
        copy.start()

    def fill(dense, gathered, live_of, j):
        count = jnp.int32(0)
        for e in range(row_blocks):
            for b in range(col_blocks):
                live = live_of[j, e, b]
                dense[e * TILE:(e + 1) * TILE, b * TILE:(b + 1) * TILE] = gathered[jnp.where(live != 0, count, CAP)]
                count = count + live

    mask_swap.wait_recv()
    lam_swap.wait_recv()
    for k in range(n):
        if k:
            copies[k].wait_recv()
        swaps[k].start()
        fill(dense_m, mine[k], mask, src[k])
        acc[...] = jnp.dot(lam_m[src[k]], dense_m[...], preferred_element_type=f32)
        swaps[k].wait_recv()
        fill(dense_t, theirs[k], other, src[k])
        out[0, src[k]] = (acc[...] + jnp.dot(
            lam_t[src[k]], dense_t[...], preferred_element_type=f32)).astype(bf16)

    for copy in t_copies + copies[1:] + swaps + [mask_swap, lam_swap]:
        copy.wait_send()


def body(n, lambda_amps, screened_ints, half_ints, singles, block_mask):
    wide, pairs, rows, half = lambda_amps.shape
    full = screened_ints.shape[2]
    inner, width = singles.shape
    row_blocks, col_blocks = half // TILE, full // TILE
    blocks = row_blocks * col_blocks
    bf16, f32 = jnp.bfloat16, jnp.float32
    dma = pltpu.SemaphoreType.DMA
    grid = n == 4
    tile = (TILE, TILE)
    lams = [pltpu.VMEM((pairs, rows, half), bf16)] * 2
    work = [pltpu.VMEM((half, full), bf16)] * 2 + [pltpu.VMEM((rows, full), f32)] + [
        pltpu.SMEM(block_mask.shape, jnp.int32)] * 2
    held = [pltpu.VMEM((CAP + 1,) + tile, bf16)] * (2 * n)
    if grid:
        raw = CAP // row_blocks
        chunks = 8
        scratch = lams + [
            pltpu.VMEM((blocks,) + tile, bf16), pltpu.VMEM((row_blocks, TILE, inner), bf16),
            pltpu.VMEM((col_blocks, inner, TILE), bf16), pltpu.VMEM((blocks,) + tile, bf16),
        ] + work + [
            dma((2 + width // TILE + row_blocks,)), dma((blocks,)), dma((n,)), dma((n,)), dma((n,)), dma((n,)),
            dma((n, chunks)), dma((n, chunks)), dma((chunks,)), dma((n, chunks)), dma((n, chunks)), dma((2,)), dma((2,)),
        ] + held + [pltpu.VMEM((raw + 1,) + tile, bf16)] * (2 * n)
    else:
        scratch = lams + [
            pltpu.VMEM((half, full), bf16), pltpu.VMEM((half, inner), bf16), pltpu.VMEM((n, inner, width), bf16),
            pltpu.VMEM((blocks,) + tile, bf16),
        ] + work + [dma((5,)), dma((n,)), dma((n,)), dma((n,)), dma((n,)), dma((n,)), dma((n,)), dma((2,)), dma((2,))] + held
    return pl.pallas_call(
        grid_kernel if grid else functools.partial(ring_kernel, n),
        out_shape=pltpu.VMEM((1, pairs, rows, full), bf16),
        in_specs=[pl.BlockSpec(memory_space=pl.ANY)] * 5,
        out_specs=pl.BlockSpec(memory_space=pltpu.VMEM),
        scratch_shapes=scratch,
        compiler_params=pltpu.CompilerParams(
            collective_id=0, has_side_effects=True, vmem_limit_bytes=56 * 1024 * 1024),
    )(lambda_amps, screened_ints, half_ints, singles, block_mask)


def solution(mesh):
    return jax.shard_map(
        functools.partial(body, mesh.shape["vir"]),
        mesh=mesh,
        in_specs=(
            P(None, "occ", "vir", "ka"),
            P(("occ", "vir"), "ka", None),
            P(("occ", "vir"), "ka", None),
            P(None, "vir"),
            P("occ", "ka", None),
        ),
        out_specs=P("ka", "occ", "vir", None),
        check_vma=False,
    )
```

time: 32.5 us -> 29.3 us (0.902)
  Pallas kernels: 31 us -> 27.8 us
    pallas_call x1, Pallas kernels: 31 us -> 27.8 us  [body(): pl.pallas_call(grid_kernel if grid else functools.partial(ring_kernel, n)...]
where the time goes in v2:
time: 29.3 us; the launch traced here: 29.1 us
  Pallas kernels  27.8 us (95%)
  local copies, waits for them, and re-layouts  1.32 us (5%)
    pallas_call x1, Pallas kernels, body(): pl.pallas_call(grid_kernel if grid else functools.partial(ring_kernel, n)...  27.8 us
    unnamed x1, local copies, waits for them, and re-layouts  1.32 us

profile of v2, /device:TPU:0, one launch (start us, length us, event | category | flops | bytes accessed | tf_op | source)
XLA Modules:
  0.0 29.1 jit_solution(12807203635357007897)
XLA Ops:
  0.0 27.8 %shard_map.55 = bf16[1,4,256,1024]{3,2,1,0:T(8,128)(2,1)S(1)} custom-call(bf16[2,4,256,512]{3,2,1,0:T(8,128)(2,1)} %lam.1, bf16[1,512,1024]{2,1,0:T(8,128)(2,1)} %x.1, bf16[1,512,128]{2,1,0:T(8,128)(2,1)} %y.1, bf16[128,256]{1,0:T(8,128)(2,1)} %t.1, s32[4,4,8]{2,1,0:T(4,128)} %mask_any.1), custom_call_target="tpu_custom_call" | custom-call | tf_op jit(solution)/shard_map/pallas_call | solution.py:424
  27.8 1.3 %copy.7 = bf16[1,4,256,1024]{3,2,1,0:T(8,128)(2,1)} copy(bf16[1,4,256,1024]{3,2,1,0:T(8,128)(2,1)S(1)} %shard_map.55) | data formatting | bytes 4194304

commit v3 on v2

--- a/solution.py
+++ b/solution.py
@@ -66,7 +66,7 @@
 
 
 def grid_kernel(lam, x, y, t, mask_any, out, lam_m, lam_t, x_v, y_v, t_v, dressed, dense_m, dense_t, acc, mask, other,
-                in_sem, x_sem, t_send, t_recv, td_send, td_recv, b_send, b_recv, f_send, d_send, d_recv, l_send, l_recv,
+                in_sem, t_send, t_recv, td_send, td_recv, b_send, b_recv, f_send, d_send, d_recv, r_recv, l_send, l_recv,
                 *bufs):
     n = 4
     mine, theirs, raw_m, raw_t = bufs[:n], bufs[n:2 * n], bufs[2 * n:3 * n], bufs[3 * n:]
@@ -87,13 +87,14 @@
         return x.at[0, pl.ds(e * TILE, TILE), pl.ds(b * TILE, TILE)]
 
     mask_load = pltpu.make_async_copy(mask_any, mask, in_sem.at[0])
+    t_own = t_v.at[pl.ds(v * cols, cols)]
     t_loads = [pltpu.make_async_copy(
-        t.at[:, pl.ds(i * TILE, TILE)], t_v.at[v * cols + i], in_sem.at[1 + i]) for i in range(cols)]
+        t.at[:, pl.ds(i * TILE, TILE)], t_v.at[v * cols + i], in_sem.at[1]) for i in range(cols)]
     y_loads = [pltpu.make_async_copy(
-        y.at[0, pl.ds(e * TILE, TILE)], y_v.at[e], in_sem.at[1 + cols + e]) for e in range(row_blocks)]
+        y.at[0, pl.ds(e * TILE, TILE)], y_v.at[e], in_sem.at[2]) for e in range(row_blocks)]
     x_loads = [pltpu.make_async_copy(
-        block(p // col_blocks, p % col_blocks), x_v.at[p], x_sem.at[p]) for p in range(row_blocks * col_blocks)]
-    lam_load = pltpu.make_async_copy(lam.at[c], lam_m, in_sem.at[1 + cols + row_blocks])
+        block(p // col_blocks, p % col_blocks), x_v.at[p], in_sem.at[3]) for p in range(row_blocks * col_blocks)]
+    lam_load = pltpu.make_async_copy(lam.at[c], lam_m, in_sem.at[4])
     mask_load.start()
     for load in t_loads + y_loads + x_loads:
         load.start()
@@ -110,23 +111,26 @@
     mask_load.wait()
     lead = top_row(mask, v, row_blocks, col_blocks)
     lead_columns = raw_columns(mask, v, lead, raw, col_blocks)
-    for load in t_loads:
-        load.wait()
+    pltpu.make_async_copy(t_own, t_own, in_sem.at[1]).wait()
     pl.semaphore_wait(barrier, 3)
 
     def t_part(k):
-        return t_v.at[pl.ds(ids[k] * cols, cols), pl.ds(pl.multiple_of(c * part, part), part)]
-
-    t_copies = [None] + [remote(t_part(0), t_part(0), t_send.at[k], t_recv.at[k], near[k]) for k in (1, 2)]
-    t_relay = remote(t_part(1), t_part(1), t_send.at[3], t_recv.at[3], to_y)
-    t_swaps = [None] + [remote(t_part(k), t_part(k), td_send.at[k], td_recv.at[k], to_core) for k in (1, 2, 3)]
-    for k in (1, 2):
-        t_copies[k].start()
+        return t_v.at[pl.ds(ids[k] * cols, cols)]
+
+    t_copies = [None] + [remote(t_part(0), t_part(0), t_send.at[0], t_recv.at[k], near[k]) for k in (1, 2)]
+    t_relay = remote(t_part(1), t_part(1), t_send.at[0], t_recv.at[0], to_y)
+    t_swaps = [None] + [remote(t_part(k), t_part(k), td_send.at[0], td_recv.at[k - 1], to_core) for k in (1, 2, 3)]
+
+    @pl.when(c == 1)
+    def _():
+        for k in (1, 2):
+            t_copies[k].start()
+
     mask_swap = remote(mask_any, other, l_send.at[0], l_recv.at[0], to_core)
     mask_swap.start()
 
-    for load in y_loads + x_loads:
-        load.wait()
+    pltpu.make_async_copy(y_v, y_v, in_sem.at[2]).wait()
+    pltpu.make_async_copy(x_v, x_v, in_sem.at[3]).wait()
     for s in range(raw):
         raw_m[0][s] = x_v[lead * col_blocks + lead_columns[s]]
     raw_m[0][raw] = y_v[lead]
@@ -136,33 +140,36 @@
     for size in [first // 2] * 2 + [late // 4] * 4:
         spans.append((at, at + size))
         at += size
-    chunks = len(spans)
     low, high = (0, 2, 4, 5), (1, 3, 6, 7)
-    paths = [None, (0, 1, 2, 3, 4, 5, 6, 7), (1, 0, 3, 2, 6, 7, 4, 5)]
-
-    def chunk(raws, gathered, k, q):
-        start, stop = spans[q]
+    groups = [(0, 0), (1, 1), (2, 2), (3, 3), (4, 5), (6, 7)]
+    paths = [None, (0, 1, 2, 3, 4, 5), (1, 0, 3, 2, 5, 4)]
+
+    def chunk(raws, gathered, k, q, r):
+        start, stop = spans[q][0], spans[r][1]
         return (raws if q < 2 else gathered)[k].at[pl.ds(start, stop - start)]
 
-    def here(k, q):
-        return chunk(raw_m, mine, k, q)
-
-    def own_copy(k, q):
-        return remote(here(0, q), here(k, q), b_send.at[k, q], b_recv.at[k, q], near[k])
+    def own_copy(k, g):
+        q, r = groups[g]
+        return remote(chunk(raw_m, mine, 0, q, r), chunk(raw_m, mine, k, q, r), b_send.at[k - 1], b_recv.at[k - 1, q], near[k])
 
     def relay_copy(k, q):
-        return remote(here(k, q), here(3, q), f_send.at[q], b_recv.at[3, q], near[3 - k])
-
-    def swap(k, q):
-        if k == 0 and q == 0:
-            return remote(mine[0].at[pl.ds(0, raw)], theirs[0].at[pl.ds(0, raw)], d_send.at[0, 0], d_recv.at[0, 0], to_core)
-        return remote(here(k, q), chunk(raw_t, theirs, k, q), d_send.at[k, q], d_recv.at[k, q], to_core)
-
-    relays = [(1, q) for q in low] + [(2, q) for q in high]
+        return remote(chunk(raw_m, mine, k, q, q), chunk(raw_m, mine, 3, q, q), f_send.at[0], b_recv.at[2, q], near[3 - k])
+
+    def swap(k, q, r):
+        return remote(chunk(raw_m, mine, k, q, r), chunk(raw_t, theirs, k, q, r), d_send.at[k],
+                      r_recv.at[k - 1] if q < 2 else d_recv.at[k], to_core)
+
+    own_swap = remote(mine[0].at[pl.ds(0, CAP)], theirs[0].at[pl.ds(0, CAP)], d_send.at[0], d_recv.at[0], to_core)
+    lam_swap = remote(lam.at[partner], lam_t, l_send.at[1], l_recv.at[1], to_core)
 
     own_copy(1, 0).start()
     own_copy(2, 1).start()
     own_copy(1, 1).start()
+
+    @pl.when(c == 0)
+    def _():
+        own_copy(2, 0).start()
+        lam_swap.start()
 
     def dress(k):
         for i in range(cols):
@@ -181,15 +188,22 @@
         order.append(place)
 
     dress(0)
-    t_copies[1].wait_recv()
-    t_relay.start()
-    own_copy(2, 0).start()
-    t_swaps[1].start()
-    t_copies[2].wait_recv()
-    t_swaps[2].start()
-    for k in (1, 2):
-        t_swaps[k].wait_recv()
-        dress(k)
+    @pl.when(c == 1)
+    def _():
+        t_copies[1].wait_recv()
+        t_relay.start()
+        own_copy(2, 0).start()
+        t_swaps[1].start()
+        t_copies[2].wait_recv()
+        t_swaps[2].start()
+
+    @pl.when(c == 0)
+    def _():
+        t_swaps[1].wait_recv()
+        t_swaps[2].wait_recv()
+
+    dress(1)
+    dress(2)
 
     def pack(q):
         for s in range(*spans[q]):
@@ -200,23 +214,26 @@
     for i in (2, 3):
         for k in (1, 2):
             own_copy(k, paths[k][i]).start()
-    t_relay.wait_recv()
-    t_swaps[3].start()
-    t_swaps[3].wait_recv()
+    @pl.when(c == 1)
+    def _():
+        t_relay.wait_recv()
+        t_swaps[3].start()
+        lam_swap.start()
+
+    @pl.when(c == 0)
+    def _():
+        t_swaps[3].wait_recv()
+
     dress(3)
-    for i in range(4, chunks):
-        if i < 6:
-            for k in (1, 2):
-                pack(paths[k][i])
+    for i in (4, 5):
+        for q in groups[i]:
+            pack(q)
+    for i in (4, 5):
         for k in (1, 2):
             own_copy(k, paths[k][i]).start()
     for s in range(raw):
         mine[0][s] = dressed[lead * col_blocks + lead_columns[s]]
-    swaps_of = [[0] + list(range(2, chunks))] + [list(range(chunks))] * 3
-    for q in swaps_of[0]:
-        swap(0, q).start()
-    lam_swap = remote(lam.at[partner], lam_t, l_send.at[1], l_recv.at[1], to_core)
-    lam_swap.start()
+    own_swap.start()
     mask_swap.wait_recv()
 
     def mend(k, raws, gathered, live_of):
@@ -227,80 +244,91 @@
             term = jnp.dot(rows, t_v[places[s]], preferred_element_type=f32)
             gathered[k][s] = (raws[k][s].astype(f32) - term).astype(bf16)
 
-    def fill(dense, gathered, live_of, k):
+    def places(live_of, k):
         j = ids[k]
         best = top_row(live_of, j, row_blocks, col_blocks)
-        slots = slots_of(live_of, j, best, raw, n - 1 - j, row_blocks, col_blocks, cols)
+        return slots_of(live_of, j, best, raw, n - 1 - j, row_blocks, col_blocks, cols)
+
+    def fill(dense, gathered, slots):
         for p, slot in enumerate(slots):
             e, b = p // col_blocks, p % col_blocks
-            dense[e * TILE:(e + 1) * TILE, b * TILE:(b + 1) * TILE] = gathered[k][slot]
-
-    def own_half(k):
-        fill(dense_m, mine, mask, k)
+            dense[e * TILE:(e + 1) * TILE, b * TILE:(b + 1) * TILE] = gathered[slot]
+
+    def own_half(k, slots):
+        fill(dense_m, mine[k], slots)
         acc[...] = jnp.dot(lam_m[ids[k]], dense_m[...], preferred_element_type=f32)
 
-    def other_half(k):
-        for q in swaps_of[k]:
-            if k == 0 or q >= 2:
-                swap(k, q).wait_recv()
-        fill(dense_t, theirs, other, k)
+    def other_half(k, slots):
+        if k == 0:
+            own_swap.wait_recv()
+        else:
+            swap(k, 2, 7).wait_recv()
+        fill(dense_t, theirs[k], slots)
         out[0, ids[k]] = (acc[...] + jnp.dot(
             lam_t[ids[k]], dense_t[...], preferred_element_type=f32)).astype(bf16)
 
-    def arrive(k, q):
-        own_copy(1, q).wait_recv() if k == 1 else own_copy(2, q).wait_recv() if k == 2 else relay_copy(1, q).wait_recv()
-        if (k, q) in relays:
-            relay_copy(k, q).start()
-        swap(k, q).start()
+    def both(k):
+        own_half(k, places(mask, k))
+        other_half(k, places(other, k))
+
+    def arrive(k, g):
+        own_copy(k, g).wait_recv()
+        q, r = groups[g]
+        for piece in range(q, r + 1):
+            if piece in (low if k == 1 else high):
+                relay_copy(k, piece).start()
+        swap(k, q, r).start()
+
+    def arrive_relayed(q):
+        relay_copy(1, q).wait_recv()
+        swap(3, q, q).start()
 
     def mend_both(k):
         mend(k, raw_m, mine, mask)
-        for q in (0, 1):
-            swap(k, q).wait_recv()
+        swap(k, 0, 1).wait_recv()
         mend(k, raw_t, theirs, other)
 
     for i in (0, 1):
+        for k in (1, 2):
+            arrive(k, paths[k][i])
+    for i in (2, 3):
         for k in (1, 2):
             arrive(k, paths[k][i])
     mend_both(1)
     mend_both(2)
-    for i in (2, 3):
-        for k in (1, 2):
-            arrive(k, paths[k][i])
     lam_load.wait()
     lam_swap.wait_recv()
-    own_half(0)
-    other_half(0)
-    for i in range(4, chunks):
+    both(0)
+    for i in (4, 5):
         for k in (1, 2):
             arrive(k, paths[k][i])
-    own_half(1)
-    other_half(1)
-    arrive(3, 0)
-    arrive(3, 1)
+    both(1)
+    arrive_relayed(0)
+    arrive_relayed(1)
     mend_both(3)
-    own_half(2)
-    other_half(2)
+    both(2)
+    here, there = places(mask, 3), places(other, 3)
     for pair in zip(low[1:], high[1:]):
         for q in pair:
-            arrive(3, q)
-    own_half(3)
-    other_half(3)
-
-    for k in (1, 2):
-        t_copies[k].wait_send()
-        for q in range(chunks):
-            own_copy(k, q).wait_send()
-    t_relay.wait_send()
-    for k in (1, 2, 3):
-        t_swaps[k].wait_send()
+            arrive_relayed(q)
+    own_half(3, here)
+    other_half(3, there)
+
+    @pl.when(c == 1)
+    def _():
+        sent = remote(t_v.at[pl.ds(0, 3 * cols)], t_v.at[pl.ds(0, 3 * cols)], t_send.at[0], t_recv.at[0], to_x)
+        sent.wait_send()
+        passed = remote(t_v.at[pl.ds(0, 3 * cols)], t_v.at[pl.ds(0, 3 * cols)], td_send.at[0], td_recv.at[0], to_core)
+        passed.wait_send()
+
     mask_swap.wait_send()
     lam_swap.wait_send()
-    for k, q in relays:
-        relay_copy(k, q).wait_send()
-    for k in range(n):
-        for q in swaps_of[k]:
-            swap(k, q).wait_send()
+    for k in (1, 2):
+        remote(mine[0], mine[k], b_send.at[k - 1], b_recv.at[0, 0], near[k]).wait_send()
+    remote(mine[1], mine[3], f_send.at[0], b_recv.at[2, 0], to_y).wait_send()
+    own_swap.wait_send()
+    for k in (1, 2, 3):
+        remote(mine[k], theirs[k], d_send.at[k], d_recv.at[k], to_core).wait_send()
 
 
 def ring_kernel(n, lam, x, y, t, mask_any, out, lam_m, lam_t, x_v, y_v, t_v, dressed, dense_m, dense_t, acc, mask, other,
@@ -413,8 +441,8 @@
             pltpu.VMEM((blocks,) + tile, bf16), pltpu.VMEM((row_blocks, TILE, inner), bf16),
             pltpu.VMEM((col_blocks, inner, TILE), bf16), pltpu.VMEM((blocks,) + tile, bf16),
         ] + work + [
-            dma((2 + width // TILE + row_blocks,)), dma((blocks,)), dma((n,)), dma((n,)), dma((n,)), dma((n,)),
-            dma((n, chunks)), dma((n, chunks)), dma((chunks,)), dma((n, chunks)), dma((n, chunks)), dma((2,)), dma((2,)),
+            dma((5,)), dma((1,)), dma((3,)), dma((1,)), dma((3,)), dma((2,)), dma((3, chunks)), dma((1,)), dma((n,)), dma((n,)),
+            dma((3,)), dma((2,)), dma((2,)),
         ] + held + [pltpu.VMEM((raw + 1,) + tile, bf16)] * (2 * n)
     else:
         scratch = lams + [

time: 29.3 us -> 27.4 us (0.935)
  Pallas kernels: 27.8 us -> 25.9 us
    pallas_call x1, Pallas kernels: 27.8 us -> 25.9 us  [body(): pl.pallas_call(grid_kernel if grid else functools.partial(ring_kernel, n)...]
where the time goes in v3:
time: 27.4 us; the launch traced here: 27.2 us
  Pallas kernels  25.9 us (95%)
  local copies, waits for them, and re-layouts  1.32 us (5%)
    pallas_call x1, Pallas kernels, body(): pl.pallas_call(grid_kernel if grid else functools.partial(ring_kernel, n)...  25.9 us
    unnamed x1, local copies, waits for them, and re-layouts  1.32 us

profile of v3, /device:TPU:0, one launch (start us, length us, event | category | flops | bytes accessed | tf_op | source)
XLA Modules:
  0.0 27.2 jit_solution(16854000691046493032)
XLA Ops:
  0.0 25.9 %shard_map.55 = bf16[1,4,256,1024]{3,2,1,0:T(8,128)(2,1)S(1)} custom-call(bf16[2,4,256,512]{3,2,1,0:T(8,128)(2,1)} %lam.1, bf16[1,512,1024]{2,1,0:T(8,128)(2,1)} %x.1, bf16[1,512,128]{2,1,0:T(8,128)(2,1)} %y.1, bf16[128,256]{1,0:T(8,128)(2,1)} %t.1, s32[4,4,8]{2,1,0:T(4,128)} %mask_any.1), custom_call_target="tpu_custom_call" | custom-call | tf_op jit(solution)/shard_map/pallas_call | solution.py:452
  25.9 1.3 %copy.7 = bf16[1,4,256,1024]{3,2,1,0:T(8,128)(2,1)} copy(bf16[1,4,256,1024]{3,2,1,0:T(8,128)(2,1)S(1)} %shard_map.55) | data formatting | bytes 4194304

commit v4 on v3

--- a/solution.py
+++ b/solution.py
@@ -65,9 +65,8 @@
     return slots
 
 
-def grid_kernel(lam, x, y, t, mask_any, out, lam_m, lam_t, x_v, y_v, t_v, dressed, dense_m, dense_t, acc, mask, other,
-                in_sem, t_send, t_recv, td_send, td_recv, b_send, b_recv, f_send, d_send, d_recv, r_recv, l_send, l_recv,
-                *bufs):
+def grid_kernel(lam, x, y, t, mask_any, stage, dense_t, lam_last, acc, lam_m, lam_t, x_v, y_v, t_v, dressed, dense_m, mask, other,
+                spare, in_sem, s_sem, t_recv, b_recv, d_recv, *bufs):
     n = 4
     mine, theirs, raw_m, raw_t = bufs[:n], bufs[n:2 * n], bufs[2 * n:3 * n], bufs[3 * n:]
     v, c = lax.axis_index("vir"), lax.axis_index("ka")
@@ -81,20 +80,23 @@
     raw = CAP // row_blocks
     late = row_blocks * cols
     first = CAP - raw - late
+    lam_blocks = lam_m.shape[0] * lam_m.shape[1] * lam_m.shape[2] // (TILE * TILE)
     f32, bf16 = jnp.float32, jnp.bfloat16
 
     def block(e, b):
         return x.at[0, pl.ds(e * TILE, TILE), pl.ds(b * TILE, TILE)]
 
+    def drain(sem, count):
+        pltpu.make_async_copy(spare.at[pl.ds(0, count)], spare.at[pl.ds(0, count)], sem).wait()
+
     mask_load = pltpu.make_async_copy(mask_any, mask, in_sem.at[0])
-    t_own = t_v.at[pl.ds(v * cols, cols)]
     t_loads = [pltpu.make_async_copy(
         t.at[:, pl.ds(i * TILE, TILE)], t_v.at[v * cols + i], in_sem.at[1]) for i in range(cols)]
     y_loads = [pltpu.make_async_copy(
         y.at[0, pl.ds(e * TILE, TILE)], y_v.at[e], in_sem.at[2]) for e in range(row_blocks)]
     x_loads = [pltpu.make_async_copy(
-        block(p // col_blocks, p % col_blocks), x_v.at[p], in_sem.at[3]) for p in range(row_blocks * col_blocks)]
-    lam_load = pltpu.make_async_copy(lam.at[c], lam_m, in_sem.at[4])
+        block(p // col_blocks, p % col_blocks), x_v.at[p], in_sem.at[2]) for p in range(row_blocks * col_blocks)]
+    lam_load = pltpu.make_async_copy(lam.at[c], lam_m, in_sem.at[3])
     mask_load.start()
     for load in t_loads + y_loads + x_loads:
         load.start()
@@ -111,26 +113,25 @@
     mask_load.wait()
     lead = top_row(mask, v, row_blocks, col_blocks)
     lead_columns = raw_columns(mask, v, lead, raw, col_blocks)
-    pltpu.make_async_copy(t_own, t_own, in_sem.at[1]).wait()
+    drain(in_sem.at[1], cols)
     pl.semaphore_wait(barrier, 3)
 
     def t_part(k):
         return t_v.at[pl.ds(ids[k] * cols, cols)]
 
-    t_copies = [None] + [remote(t_part(0), t_part(0), t_send.at[0], t_recv.at[k], near[k]) for k in (1, 2)]
-    t_relay = remote(t_part(1), t_part(1), t_send.at[0], t_recv.at[0], to_y)
-    t_swaps = [None] + [remote(t_part(k), t_part(k), td_send.at[0], td_recv.at[k - 1], to_core) for k in (1, 2, 3)]
+    t_copies = [None] + [remote(t_part(0), t_part(0), s_sem.at[1], t_recv.at[k], near[k]) for k in (1, 2)]
+    t_relay = remote(t_part(1), t_part(1), s_sem.at[1], t_recv.at[0], to_y)
+    t_swaps = [None] + [remote(t_part(k), t_part(k), s_sem.at[1], d_recv.at[k // 3], to_core) for k in (1, 2, 3)]
 
     @pl.when(c == 1)
     def _():
         for k in (1, 2):
             t_copies[k].start()
 
-    mask_swap = remote(mask_any, other, l_send.at[0], l_recv.at[0], to_core)
+    mask_swap = remote(mask_any, other, s_sem.at[2], d_recv.at[2], to_core)
     mask_swap.start()
 
-    pltpu.make_async_copy(y_v, y_v, in_sem.at[2]).wait()
-    pltpu.make_async_copy(x_v, x_v, in_sem.at[3]).wait()
+    drain(in_sem.at[2], row_blocks + row_blocks * col_blocks)
     for s in range(raw):
         raw_m[0][s] = x_v[lead * col_blocks + lead_columns[s]]
     raw_m[0][raw] = y_v[lead]
@@ -148,19 +149,24 @@
         start, stop = spans[q][0], spans[r][1]
         return (raws if q < 2 else gathered)[k].at[pl.ds(start, stop - start)]
 
+    stages = (0, 0, 1, 1, 2, 2)
+    last_stages = (0, 0, 1, 1, 2, 3, 2, 3)
+    sizes = [raw + 1, first, late, late // 2]
+
     def own_copy(k, g):
         q, r = groups[g]
-        return remote(chunk(raw_m, mine, 0, q, r), chunk(raw_m, mine, k, q, r), b_send.at[k - 1], b_recv.at[k - 1, q], near[k])
+        return remote(chunk(raw_m, mine, 0, q, r), chunk(raw_m, mine, k, q, r), s_sem.at[0], b_recv.at[k - 1, stages[g]], near[k])
 
     def relay_copy(k, q):
-        return remote(chunk(raw_m, mine, k, q, q), chunk(raw_m, mine, 3, q, q), f_send.at[0], b_recv.at[2, q], near[3 - k])
+        return remote(chunk(raw_m, mine, k, q, q), chunk(raw_m, mine, 3, q, q), s_sem.at[0],
+                      b_recv.at[2, last_stages[q]], near[3 - k])
 
     def swap(k, q, r):
-        return remote(chunk(raw_m, mine, k, q, r), chunk(raw_t, theirs, k, q, r), d_send.at[k],
-                      r_recv.at[k - 1] if q < 2 else d_recv.at[k], to_core)
-
-    own_swap = remote(mine[0].at[pl.ds(0, CAP)], theirs[0].at[pl.ds(0, CAP)], d_send.at[0], d_recv.at[0], to_core)
-    lam_swap = remote(lam.at[partner], lam_t, l_send.at[1], l_recv.at[1], to_core)
+        return remote(chunk(raw_m, mine, k, q, r), chunk(raw_t, theirs, k, q, r), s_sem.at[0],
+                      d_recv.at[3 + k // 3] if q < 2 else d_recv.at[5 + k], to_core)
+
+    own_swap = remote(mine[0].at[pl.ds(0, CAP)], theirs[0].at[pl.ds(0, CAP)], s_sem.at[0], d_recv.at[5], to_core)
+    lam_swap = remote(lam.at[partner], lam_t, s_sem.at[0], d_recv.at[5], to_core)
 
     own_copy(1, 0).start()
     own_copy(2, 1).start()
@@ -199,8 +205,7 @@
 
     @pl.when(c == 0)
     def _():
-        t_swaps[1].wait_recv()
-        t_swaps[2].wait_recv()
+        drain(d_recv.at[0], 2 * cols)
 
     dress(1)
     dress(2)
@@ -259,76 +264,82 @@
         acc[...] = jnp.dot(lam_m[ids[k]], dense_m[...], preferred_element_type=f32)
 
     def other_half(k, slots):
-        if k == 0:
-            own_swap.wait_recv()
-        else:
-            swap(k, 2, 7).wait_recv()
+        if k:
+            drain(d_recv.at[5 + k], CAP - raw)
         fill(dense_t, theirs[k], slots)
-        out[0, ids[k]] = (acc[...] + jnp.dot(
-            lam_t[ids[k]], dense_t[...], preferred_element_type=f32)).astype(bf16)
+        if k < n - 1:
+            stage[k] = (acc[...] + jnp.dot(
+                lam_t[ids[k]], dense_t[...], preferred_element_type=f32)).astype(bf16)
 
     def both(k):
         own_half(k, places(mask, k))
         other_half(k, places(other, k))
 
-    def arrive(k, g):
-        own_copy(k, g).wait_recv()
-        q, r = groups[g]
-        for piece in range(q, r + 1):
-            if piece in (low if k == 1 else high):
-                relay_copy(k, piece).start()
-        swap(k, q, r).start()
-
-    def arrive_relayed(q):
-        relay_copy(1, q).wait_recv()
-        swap(3, q, q).start()
-
-    def mend_both(k):
-        mend(k, raw_m, mine, mask)
-        swap(k, 0, 1).wait_recv()
-        mend(k, raw_t, theirs, other)
-
-    for i in (0, 1):
-        for k in (1, 2):
-            arrive(k, paths[k][i])
-    for i in (2, 3):
-        for k in (1, 2):
-            arrive(k, paths[k][i])
-    mend_both(1)
-    mend_both(2)
+    def arrive(k, level):
+        drain(b_recv.at[k - 1, level], sizes[level])
+        for q in (low if k == 1 else high):
+            if min(last_stages[q], 2) == level:
+                relay_copy(k, q).start()
+        swap(k, *((0, 1), (2, 3), (4, 7))[level]).start()
+
+    arrive(1, 0)
+    arrive(2, 0)
+    arrive(1, 1)
+    arrive(2, 1)
+    mend(1, raw_m, mine, mask)
+    mend(2, raw_m, mine, mask)
+    drain(d_recv.at[3], 2 * (raw + 1))
+    mend(1, raw_t, theirs, other)
+    mend(2, raw_t, theirs, other)
     lam_load.wait()
-    lam_swap.wait_recv()
+    drain(d_recv.at[5], CAP + lam_blocks)
     both(0)
-    for i in (4, 5):
-        for k in (1, 2):
-            arrive(k, paths[k][i])
+    arrive(1, 2)
+    arrive(2, 2)
     both(1)
-    arrive_relayed(0)
-    arrive_relayed(1)
-    mend_both(3)
+    drain(b_recv.at[2, 0], raw + 1)
+    swap(3, 0, 1).start()
+    mend(3, raw_m, mine, mask)
+    drain(d_recv.at[4], raw + 1)
+    mend(3, raw_t, theirs, other)
     both(2)
+    lam_last[...] = lam_t[ids[3]]
     here, there = places(mask, 3), places(other, 3)
-    for pair in zip(low[1:], high[1:]):
-        for q in pair:
-            arrive_relayed(q)
+    drain(b_recv.at[2, 1], first)
+    swap(3, 2, 3).start()
+    for level in (2, 3):
+        drain(b_recv.at[2, level], late // 2)
+        for q in (2 + level, 4 + level):
+            swap(3, q, q).start()
     own_half(3, here)
     other_half(3, there)
 
     @pl.when(c == 1)
     def _():
-        sent = remote(t_v.at[pl.ds(0, 3 * cols)], t_v.at[pl.ds(0, 3 * cols)], t_send.at[0], t_recv.at[0], to_x)
-        sent.wait_send()
-        passed = remote(t_v.at[pl.ds(0, 3 * cols)], t_v.at[pl.ds(0, 3 * cols)], td_send.at[0], td_recv.at[0], to_core)
-        passed.wait_send()
+        drain(s_sem.at[1], 6 * cols)
 
     mask_swap.wait_send()
-    lam_swap.wait_send()
-    for k in (1, 2):
-        remote(mine[0], mine[k], b_send.at[k - 1], b_recv.at[0, 0], near[k]).wait_send()
-    remote(mine[1], mine[3], f_send.at[0], b_recv.at[2, 0], to_y).wait_send()
-    own_swap.wait_send()
-    for k in (1, 2, 3):
-        remote(mine[k], theirs[k], d_send.at[k], d_recv.at[k], to_core).wait_send()
+    drain(s_sem.at[0], 3 * (CAP + 1) + CAP + 3 * (CAP + 1) + lam_blocks)
+
+
+def last_kernel(done, dense_t, lam_last, acc, out, stage, sems):
+    v = lax.axis_index("vir")
+    row, col = v // 2, v % 2
+    ids = [v, row * 2 + (1 - col), (1 - row) * 2 + col, 3 - v]
+    count = done.shape[0]
+    pieces, rows, width = stage.shape
+    copies = [pltpu.make_async_copy(done.at[k], out.at[0, ids[k]], sems.at[pieces + k]) for k in range(count)]
+    for copy in copies:
+        copy.start()
+    for i in range(pieces):
+        columns = slice(i * width, (i + 1) * width)
+        stage[i] = (acc[:, columns] + jnp.dot(
+            lam_last[...], dense_t[:, columns], preferred_element_type=jnp.float32)).astype(jnp.bfloat16)
+        copy = pltpu.make_async_copy(stage.at[i], out.at[0, ids[3], :, pl.ds(i * width, width)], sems.at[i])
+        copy.start()
+        copies.append(copy)
+    for copy in copies:
+        copy.wait()
 
 
 def ring_kernel(n, lam, x, y, t, mask_any, out, lam_m, lam_t, x_v, y_v, t_v, dressed, dense_m, dense_t, acc, mask, other,
@@ -428,36 +439,51 @@
     blocks = row_blocks * col_blocks
     bf16, f32 = jnp.bfloat16, jnp.float32
     dma = pltpu.SemaphoreType.DMA
-    grid = n == 4
     tile = (TILE, TILE)
+    anywhere, vmem = pl.BlockSpec(memory_space=pl.ANY), pl.BlockSpec(memory_space=pltpu.VMEM)
     lams = [pltpu.VMEM((pairs, rows, half), bf16)] * 2
-    work = [pltpu.VMEM((half, full), bf16)] * 2 + [pltpu.VMEM((rows, full), f32)] + [
-        pltpu.SMEM(block_mask.shape, jnp.int32)] * 2
+    dense, total = pltpu.VMEM((half, full), bf16), pltpu.VMEM((rows, full), f32)
+    masks = [pltpu.SMEM(block_mask.shape, jnp.int32)] * 2
     held = [pltpu.VMEM((CAP + 1,) + tile, bf16)] * (2 * n)
-    if grid:
-        raw = CAP // row_blocks
-        chunks = 8
-        scratch = lams + [
+    args = (lambda_amps, screened_ints, half_ints, singles, block_mask)
+    params = pltpu.CompilerParams(collective_id=0, has_side_effects=True, vmem_limit_bytes=56 * 1024 * 1024)
+    if n != 4:
+        return pl.pallas_call(
+            functools.partial(ring_kernel, n),
+            out_shape=pltpu.VMEM((1, pairs, rows, full), bf16),
+            in_specs=[anywhere] * 5,
+            out_specs=vmem,
+            scratch_shapes=lams + [
+                pltpu.VMEM((half, full), bf16), pltpu.VMEM((half, inner), bf16), pltpu.VMEM((n, inner, width), bf16),
+                pltpu.VMEM((blocks,) + tile, bf16), dense, dense, total,
+            ] + masks + [dma((5,)), dma((n,)), dma((n,)), dma((n,)), dma((n,)), dma((n,)), dma((n,)), dma((2,)), dma((2,))] + held,
+            compiler_params=params,
+        )(*args)
+    raw = CAP // row_blocks
+    held_over = (pltpu.VMEM((n - 1, rows, full), bf16), dense, pltpu.VMEM((rows, half), bf16), total)
+    handed = pl.pallas_call(
+        grid_kernel,
+        out_shape=held_over,
+        in_specs=[anywhere] * 5,
+        out_specs=(vmem,) * 4,
+        scratch_shapes=lams + [
             pltpu.VMEM((blocks,) + tile, bf16), pltpu.VMEM((row_blocks, TILE, inner), bf16),
-            pltpu.VMEM((col_blocks, inner, TILE), bf16), pltpu.VMEM((blocks,) + tile, bf16),
-        ] + work + [
-            dma((5,)), dma((1,)), dma((3,)), dma((1,)), dma((3,)), dma((2,)), dma((3, chunks)), dma((1,)), dma((n,)), dma((n,)),
-            dma((3,)), dma((2,)), dma((2,)),
-        ] + held + [pltpu.VMEM((raw + 1,) + tile, bf16)] * (2 * n)
-    else:
-        scratch = lams + [
-            pltpu.VMEM((half, full), bf16), pltpu.VMEM((half, inner), bf16), pltpu.VMEM((n, inner, width), bf16),
-            pltpu.VMEM((blocks,) + tile, bf16),
-        ] + work + [dma((5,)), dma((n,)), dma((n,)), dma((n,)), dma((n,)), dma((n,)), dma((n,)), dma((2,)), dma((2,))] + held
+            pltpu.VMEM((col_blocks, inner, TILE), bf16), pltpu.VMEM((blocks,) + tile, bf16), dense,
+        ] + masks + [
+            pltpu.VMEM((7 * (CAP + 1) + pairs * rows * half // (TILE * TILE),) + tile, bf16),
+            dma((4,)), dma((3,)), dma((3,)), dma((3, 4)), dma((9,)),
+        ] + held + [pltpu.VMEM((raw + 1,) + tile, bf16)] * (2 * n),
+        compiler_params=params,
+    )(*args)
+    pieces = 2
     return pl.pallas_call(
-        grid_kernel if grid else functools.partial(ring_kernel, n),
-        out_shape=pltpu.VMEM((1, pairs, rows, full), bf16),
-        in_specs=[pl.BlockSpec(memory_space=pl.ANY)] * 5,
-        out_specs=pl.BlockSpec(memory_space=pltpu.VMEM),
-        scratch_shapes=scratch,
-        compiler_params=pltpu.CompilerParams(
-            collective_id=0, has_side_effects=True, vmem_limit_bytes=56 * 1024 * 1024),
-    )(lambda_amps, screened_ints, half_ints, singles, block_mask)
+        last_kernel,
+        out_shape=jax.ShapeDtypeStruct((1, pairs, rows, full), bf16),
+        in_specs=[vmem] * 4,
+        out_specs=anywhere,
+        scratch_shapes=[pltpu.VMEM((pieces, rows, full // pieces), bf16), dma((pieces + n - 1,))],
+        compiler_params=pltpu.CompilerParams(vmem_limit_bytes=8 * 1024 * 1024),
+    )(*handed)
 
 
 def solution(mesh):

time: 27.4 us -> 27 us (0.985)
  local copies, waits for them, and re-layouts: 1.32 us -> 0 us
  Pallas kernels: 25.9 us -> 26.8 us
    unnamed x1 -> x0, local copies, waits for them, and re-layouts: 1.32 us -> none
    pallas_call x1 -> x2, Pallas kernels: 25.9 us -> 26.8 us  [the longest x1 25.4 us: body(): pl.pallas_call(grid_kernel, out_shape=held_over, in_specs=[anywhere] * 5,...]
where the time goes in v4:
time: 27 us; the launch traced here: 26.8 us
  Pallas kernels  26.8 us (99%)
    pallas_call x1, Pallas kernels, body(): pl.pallas_call(grid_kernel, out_shape=held_over, in_specs=[anywhere] * 5,...  25.4 us
    pallas_call x1, Pallas kernels, body(): pl.pallas_call(last_kernel, out_shape=jax.ShapeDtypeStruct((1, pairs, row...  1.39 us

profile of v4, /device:TPU:0, one launch (start us, length us, event | category | flops | bytes accessed | tf_op | source)
XLA Modules:
  0.0 26.8 jit_solution(18441464254201812192)
XLA Ops:
  0.0 25.4 %shard_map.55 = (bf16[3,256,1024]{2,1,0:T(8,128)(2,1)S(1)}, bf16[512,1024]{1,0:T(8,128)(2,1)S(1)}, bf16[256,512]{1,0:T(8,128)(2,1)S(1)}, f32[256,1024]{1,0:T(8,128)S(1)}) custom-call(bf16[2,4,256,512]{3,2,1,0:T(8,128)(2,1)} %lam.1, bf16[1,512,1024]{2,1,0:T(8,128)(2,1)} %x.1, bf16[1,512,128]{2,1,0:T(8,128)(2,1)} %y.1, bf16[128,256]{1,0:T(8,128)(2,1)} %t.1, ...), custom_call_target="tpu_custom_call" | custom-call | tf_op jit(solution)/shard_map/pallas_call | solution.py:464
  25.4 1.4 %shard_map.56 = bf16[1,4,256,1024]{3,2,1,0:T(8,128)(2,1)} custom-call(bf16[3,256,1024]{2,1,0:T(8,128)(2,1)S(1)} %get-tuple-element.9.done, bf16[512,1024]{1,0:T(8,128)(2,1)S(1)} %get-tuple-element.10.dense_t, bf16[256,512]{1,0:T(8,128)(2,1)S(1)} %get-tuple-element.11.lam_last, f32[256,1024]{1,0:T(8,128)S(1)} %get-tuple-element.12.acc), custom_call_target="tpu_custom_call" | custom-call | tf_op jit(solution)/shard_map/pallas_call | solution.py:479

commit v5 on v4

--- a/solution.py
+++ b/solution.py
@@ -65,8 +65,8 @@
     return slots
 
 
-def grid_kernel(lam, x, y, t, mask_any, stage, dense_t, lam_last, acc, lam_m, lam_t, x_v, y_v, t_v, dressed, dense_m, mask, other,
-                spare, in_sem, s_sem, t_recv, b_recv, d_recv, *bufs):
+def grid_kernel(lam, x, y, t, mask_any, stage, dense_t, lam_last, acc, lam_m, lam_t, x_v, y_v, t_v, dressed, mask, other,
+                tail, spare, in_sem, s_sem, t_recv, b_recv, d_recv, ready, *bufs):
     n = 4
     mine, theirs, raw_m, raw_t = bufs[:n], bufs[n:2 * n], bufs[2 * n:3 * n], bufs[3 * n:]
     v, c = lax.axis_index("vir"), lax.axis_index("ka")
@@ -83,6 +83,15 @@
     lam_blocks = lam_m.shape[0] * lam_m.shape[1] * lam_m.shape[2] // (TILE * TILE)
     f32, bf16 = jnp.float32, jnp.bfloat16
 
+    to_x, to_y, to_core = {"vir": ids[1]}, {"vir": ids[2]}, {"ka": partner}
+    near = [None, to_x, to_y]
+    last = [None, col == 1, row == 1]
+    barrier = enter([to_core])
+    for k in (1, 2):
+        @pl.when(jnp.logical_not(last[k]))
+        def _():
+            pl.semaphore_signal(barrier, inc=1, device_id=near[k], device_id_type=MESH)
+
     def block(e, b):
         return x.at[0, pl.ds(e * TILE, TILE), pl.ds(b * TILE, TILE)]
 
@@ -96,49 +105,51 @@
         y.at[0, pl.ds(e * TILE, TILE)], y_v.at[e], in_sem.at[2]) for e in range(row_blocks)]
     x_loads = [pltpu.make_async_copy(
         block(p // col_blocks, p % col_blocks), x_v.at[p], in_sem.at[2]) for p in range(row_blocks * col_blocks)]
-    lam_load = pltpu.make_async_copy(lam.at[c], lam_m, in_sem.at[3])
+    lam_load = pltpu.make_async_copy(lam.at[c], lam_m, d_recv.at[5])
     mask_load.start()
     for load in t_loads + y_loads + x_loads:
         load.start()
-    lam_load.start()
-    to_x, to_y, to_core = {"vir": ids[1]}, {"vir": ids[2]}, {"ka": partner}
-    near = [None, to_x, to_y]
-    barrier = enter([to_x, to_y, to_core])
 
     zero = jnp.zeros((TILE, TILE), bf16)
     for k in range(n):
         mine[k][CAP] = zero
         theirs[k][CAP] = zero
+    tail[2] = zero
+
+    pl.semaphore_wait(barrier, 1 + row + col)
+    for k in (1, 2):
+        @pl.when(last[k])
+        def _():
+            pl.semaphore_signal(ready.at[k - 1], inc=1, device_id=near[k], device_id_type=MESH)
 
     mask_load.wait()
     lead = top_row(mask, v, row_blocks, col_blocks)
     lead_columns = raw_columns(mask, v, lead, raw, col_blocks)
     drain(in_sem.at[1], cols)
-    pl.semaphore_wait(barrier, 3)
-
     def t_part(k):
         return t_v.at[pl.ds(ids[k] * cols, cols)]
 
-    t_copies = [None] + [remote(t_part(0), t_part(0), s_sem.at[1], t_recv.at[k], near[k]) for k in (1, 2)]
+    t_copies = [None] + [remote(t_part(0), t_part(0), s_sem.at[1], t_recv.at[1], near[k]) for k in (1, 2)]
     t_relay = remote(t_part(1), t_part(1), s_sem.at[1], t_recv.at[0], to_y)
     t_swaps = [None] + [remote(t_part(k), t_part(k), s_sem.at[1], d_recv.at[k // 3], to_core) for k in (1, 2, 3)]
 
-    @pl.when(c == 1)
-    def _():
-        for k in (1, 2):
+    for k in (1, 2):
+        @pl.when((c == 1) & last[k])
+        def _():
             t_copies[k].start()
 
     mask_swap = remote(mask_any, other, s_sem.at[2], d_recv.at[2], to_core)
     mask_swap.start()
 
     drain(in_sem.at[2], row_blocks + row_blocks * col_blocks)
+    lam_load.start()
     for s in range(raw):
         raw_m[0][s] = x_v[lead * col_blocks + lead_columns[s]]
     raw_m[0][raw] = y_v[lead]
 
     spans = [(0, raw // 2), (raw // 2, raw + 1)]
     at = raw
-    for size in [first // 2] * 2 + [late // 4] * 4:
+    for size in [first // 2] * 2 + [late // 2 - 1, 1] * 2:
         spans.append((at, at + size))
         at += size
     low, high = (0, 2, 4, 5), (1, 3, 6, 7)
@@ -151,30 +162,49 @@
 
     stages = (0, 0, 1, 1, 2, 2)
     last_stages = (0, 0, 1, 1, 2, 3, 2, 3)
-    sizes = [raw + 1, first, late, late // 2]
+    sizes = [raw + 1, first, late]
 
     def own_copy(k, g):
         q, r = groups[g]
-        return remote(chunk(raw_m, mine, 0, q, r), chunk(raw_m, mine, k, q, r), s_sem.at[0], b_recv.at[k - 1, stages[g]], near[k])
+        return remote(chunk(raw_m, mine, 0, q, r), chunk(raw_m, mine, k, q, r), s_sem.at[0], b_recv.at[stages[g]], near[k])
 
     def relay_copy(k, q):
         return remote(chunk(raw_m, mine, k, q, q), chunk(raw_m, mine, 3, q, q), s_sem.at[0],
-                      b_recv.at[2, last_stages[q]], near[3 - k])
+                      b_recv.at[3 + last_stages[q]], near[3 - k])
 
     def swap(k, q, r):
-        return remote(chunk(raw_m, mine, k, q, r), chunk(raw_t, theirs, k, q, r), s_sem.at[0],
-                      d_recv.at[3 + k // 3] if q < 2 else d_recv.at[5 + k], to_core)
+        sem = 3 + k // 3 if q < 2 else 6 if k < 3 else 8 if q in (5, 7) else 7
+        target = tail.at[pl.ds(q // 7, 1)] if k == 3 and q in (5, 7) else chunk(raw_t, theirs, k, q, r)
+        return remote(chunk(raw_m, mine, k, q, r), target, s_sem.at[0], d_recv.at[sem], to_core)
 
     own_swap = remote(mine[0].at[pl.ds(0, CAP)], theirs[0].at[pl.ds(0, CAP)], s_sem.at[0], d_recv.at[5], to_core)
     lam_swap = remote(lam.at[partner], lam_t, s_sem.at[0], d_recv.at[5], to_core)
 
-    own_copy(1, 0).start()
-    own_copy(2, 1).start()
-    own_copy(1, 1).start()
+    def raw_start(k):
+        own_copy(k, paths[k][0]).start()
+
+        @pl.when((c == 0) | (k == 1))
+        def _():
+            own_copy(k, paths[k][1]).start()
+
+    for k in (1, 2):
+        @pl.when(last[k])
+        def _():
+            raw_start(k)
+
+    for k in (1, 2):
+        @pl.when(jnp.logical_not(last[k]))
+        def _():
+            pl.semaphore_wait(ready.at[k - 1], 1)
+
+            @pl.when(c == 1)
+            def _():
+                t_copies[k].start()
+
+            raw_start(k)
 
     @pl.when(c == 0)
     def _():
-        own_copy(2, 0).start()
         lam_swap.start()
 
     def dress(k):
@@ -196,11 +226,10 @@
     dress(0)
     @pl.when(c == 1)
     def _():
-        t_copies[1].wait_recv()
+        drain(t_recv.at[1], 2 * cols)
         t_relay.start()
         own_copy(2, 0).start()
         t_swaps[1].start()
-        t_copies[2].wait_recv()
         t_swaps[2].start()
 
     @pl.when(c == 0)
@@ -254,65 +283,89 @@
         best = top_row(live_of, j, row_blocks, col_blocks)
         return slots_of(live_of, j, best, raw, n - 1 - j, row_blocks, col_blocks, cols)
 
-    def fill(dense, gathered, slots):
-        for p, slot in enumerate(slots):
-            e, b = p // col_blocks, p % col_blocks
-            dense[e * TILE:(e + 1) * TILE, b * TILE:(b + 1) * TILE] = gathered[slot]
-
-    def own_half(k, slots):
-        fill(dense_m, mine[k], slots)
-        acc[...] = jnp.dot(lam_m[ids[k]], dense_m[...], preferred_element_type=f32)
-
-    def other_half(k, slots):
-        if k:
-            drain(d_recv.at[5 + k], CAP - raw)
-        fill(dense_t, theirs[k], slots)
-        if k < n - 1:
-            stage[k] = (acc[...] + jnp.dot(
-                lam_t[ids[k]], dense_t[...], preferred_element_type=f32)).astype(bf16)
+    def tile(gathered, slots, e, b):
+        rows = [jnp.concatenate([gathered[slots[p * col_blocks + q]] for q in (b, b + 1)], axis=1) for p in (e, e + 1)]
+        return jnp.concatenate(rows, axis=0)
+
+    def product(pairs, b):
+        return sum(
+            jnp.dot(rows[:, e * TILE:(e + 2) * TILE], tile(gathered, slots, e, b), preferred_element_type=f32)
+            for rows, gathered, slots in pairs for e in range(0, row_blocks, 2))
 
     def both(k):
-        own_half(k, places(mask, k))
-        other_half(k, places(other, k))
-
-    def arrive(k, level):
-        drain(b_recv.at[k - 1, level], sizes[level])
-        for q in (low if k == 1 else high):
-            if min(last_stages[q], 2) == level:
-                relay_copy(k, q).start()
-        swap(k, *((0, 1), (2, 3), (4, 7))[level]).start()
-
-    arrive(1, 0)
-    arrive(2, 0)
-    arrive(1, 1)
-    arrive(2, 1)
+        mine_k = (lam_m[ids[k]], mine[k], places(mask, k))
+        theirs_k = (lam_t[ids[k]], theirs[k], places(other, k))
+        for b in range(0, col_blocks, 2):
+            stage[k, :, b * TILE:(b + 2) * TILE] = product([mine_k, theirs_k], b).astype(bf16)
+
+    def arrive(level):
+        drain(b_recv.at[level], 2 * sizes[level])
+        for k in (1, 2):
+            for q in (low if k == 1 else high):
+                if min(last_stages[q], 2) == level:
+                    relay_copy(k, q).start()
+        for k in (1, 2):
+            swap(k, *((0, 1), (2, 3), (4, 7))[level]).start()
+
+    arrive(0)
+    arrive(1)
     mend(1, raw_m, mine, mask)
     mend(2, raw_m, mine, mask)
     drain(d_recv.at[3], 2 * (raw + 1))
     mend(1, raw_t, theirs, other)
     mend(2, raw_t, theirs, other)
-    lam_load.wait()
-    drain(d_recv.at[5], CAP + lam_blocks)
+    drain(d_recv.at[5], CAP + 2 * lam_blocks)
     both(0)
-    arrive(1, 2)
-    arrive(2, 2)
+    arrive(2)
+    here, there = places(mask, 3), places(other, 3)
+    ends = [spans[5][0], spans[7][0]]
+    for end in ends:
+        theirs[3][end] = zero
+    seats = []
+    for end in ends:
+        seat = jnp.int32(-1)
+        for p, slot in enumerate(there):
+            seat = jnp.where(slot == end, p, seat)
+        seats.append(seat)
+    lam_rows = lam_t[ids[3]]
+    for i, seat in enumerate(seats):
+        rows = lam_rows[:, :TILE]
+        for e in range(1, row_blocks):
+            rows = jnp.where(seat >= e * col_blocks, lam_rows[:, e * TILE:(e + 1) * TILE], rows)
+        lam_last[:, i * TILE:(i + 1) * TILE] = rows
+    there = [jnp.where((slot == ends[0]) | (slot == ends[1]), CAP, slot) for slot in there]
+    picks = []
+    for i, seat in enumerate(seats):
+        for b in range(col_blocks):
+            hit = seat == b
+            for e in range(1, row_blocks):
+                hit = hit | (seat == e * col_blocks + b)
+            picks.append(jnp.where(hit, i, 2))
+    drain(b_recv.at[3], raw + 1)
+    swap(3, 0, 1).start()
+    drain(d_recv.at[6], 2 * (CAP - raw))
     both(1)
-    drain(b_recv.at[2, 0], raw + 1)
-    swap(3, 0, 1).start()
+    drain(b_recv.at[4], first)
+    swap(3, 2, 3).start()
     mend(3, raw_m, mine, mask)
     drain(d_recv.at[4], raw + 1)
     mend(3, raw_t, theirs, other)
     both(2)
-    lam_last[...] = lam_t[ids[3]]
-    here, there = places(mask, 3), places(other, 3)
-    drain(b_recv.at[2, 1], first)
-    swap(3, 2, 3).start()
-    for level in (2, 3):
-        drain(b_recv.at[2, level], late // 2)
-        for q in (2 + level, 4 + level):
-            swap(3, q, q).start()
-    own_half(3, here)
-    other_half(3, there)
+    drain(b_recv.at[5], late - 2)
+    for q in (4, 6):
+        swap(3, q, q).start()
+    drain(b_recv.at[6], 2)
+    for q in (5, 7):
+        swap(3, q, q).start()
+    for b in range(0, col_blocks, 2):
+        acc[:, b * TILE:(b + 2) * TILE] = product([(lam_m[ids[3]], mine[3], here)], b)
+    drain(d_recv.at[7], CAP - raw - 2)
+    for b in range(0, col_blocks, 2):
+        acc[:, b * TILE:(b + 2) * TILE] += product([(lam_t[ids[3]], theirs[3], there)], b)
+    drain(d_recv.at[8], 2)
+    for i, pick in enumerate(picks):
+        e, b = i // col_blocks, i % col_blocks
+        dense_t[e * TILE:(e + 1) * TILE, b * TILE:(b + 1) * TILE] = tail[pick]
 
     @pl.when(c == 1)
     def _():
@@ -460,7 +513,7 @@
             compiler_params=params,
         )(*args)
     raw = CAP // row_blocks
-    held_over = (pltpu.VMEM((n - 1, rows, full), bf16), dense, pltpu.VMEM((rows, half), bf16), total)
+    held_over = (pltpu.VMEM((n - 1, rows, full), bf16), pltpu.VMEM((2 * TILE, full), bf16), pltpu.VMEM((rows, 2 * TILE), bf16), total)
     handed = pl.pallas_call(
         grid_kernel,
         out_shape=held_over,
@@ -468,10 +521,10 @@
         out_specs=(vmem,) * 4,
         scratch_shapes=lams + [
             pltpu.VMEM((blocks,) + tile, bf16), pltpu.VMEM((row_blocks, TILE, inner), bf16),
-            pltpu.VMEM((col_blocks, inner, TILE), bf16), pltpu.VMEM((blocks,) + tile, bf16), dense,
+            pltpu.VMEM((col_blocks, inner, TILE), bf16), pltpu.VMEM((blocks,) + tile, bf16),
         ] + masks + [
-            pltpu.VMEM((7 * (CAP + 1) + pairs * rows * half // (TILE * TILE),) + tile, bf16),
-            dma((4,)), dma((3,)), dma((3,)), dma((3, 4)), dma((9,)),
+            pltpu.VMEM((3,) + tile, bf16), pltpu.VMEM((7 * (CAP + 1) + pairs * rows * half // (TILE * TILE),) + tile, bf16),
+            dma((3,)), dma((3,)), dma((2,)), dma((7,)), dma((9,)), pltpu.SemaphoreType.REGULAR((2,)),
         ] + held + [pltpu.VMEM((raw + 1,) + tile, bf16)] * (2 * n),
         compiler_params=params,
     )(*args)

time: 27 us -> 26.7 us (0.989); the launches traced: 26.8 us -> 26.2 us
  Pallas kernels: 26.8 us -> 26.2 us
    pallas_call x1, Pallas kernels: 25.4 us -> 24.7 us  [body(): pl.pallas_call(grid_kernel, out_shape=held_over, in_specs=[anywhere] * 5,...]
where the time goes in v5:
time: 26.7 us; the launch traced here: 26.2 us
  Pallas kernels  26.2 us (98%)
    pallas_call x1, Pallas kernels, body(): pl.pallas_call(grid_kernel, out_shape=held_over, in_specs=[anywhere] * 5,...  24.7 us
    pallas_call x1, Pallas kernels, body(): pl.pallas_call(last_kernel, out_shape=jax.ShapeDtypeStruct((1, pairs, row...  1.44 us

profile of v5, /device:TPU:0, one launch (start us, length us, event | category | flops | bytes accessed | tf_op | source)
XLA Modules:
  0.0 26.2 jit_solution(17086686218476584694)
XLA Ops:
  0.0 24.7 %shard_map.55 = (bf16[3,256,1024]{2,1,0:T(8,128)(2,1)S(1)}, bf16[256,1024]{1,0:T(8,128)(2,1)S(1)}, bf16[256,256]{1,0:T(8,128)(2,1)S(1)}, f32[256,1024]{1,0:T(8,128)S(1)}) custom-call(bf16[2,4,256,512]{3,2,1,0:T(8,128)(2,1)} %lam.1, bf16[1,512,1024]{2,1,0:T(8,128)(2,1)} %x.1, bf16[1,512,128]{2,1,0:T(8,128)(2,1)} %y.1, bf16[128,256]{1,0:T(8,128)(2,1)} %t.1, ...), custom_call_target="tpu_custom_call" | custom-call | tf_op jit(solution)/shard_map/pallas_call | solution.py:517
  24.7 1.4 %shard_map.56 = bf16[1,4,256,1024]{3,2,1,0:T(8,128)(2,1)} custom-call(bf16[3,256,1024]{2,1,0:T(8,128)(2,1)S(1)} %get-tuple-element.9.done, bf16[256,1024]{1,0:T(8,128)(2,1)S(1)} %get-tuple-element.10.dense_t, bf16[256,256]{1,0:T(8,128)(2,1)S(1)} %get-tuple-element.11.lam_last, f32[256,1024]{1,0:T(8,128)S(1)} %get-tuple-element.12.acc), custom_call_target="tpu_custom_call" | custom-call | tf_op jit(solution)/shard_map/pallas_call | solution.py:532

commit v6 on v5

--- a/solution.py
+++ b/solution.py
@@ -160,13 +160,13 @@
         start, stop = spans[q][0], spans[r][1]
         return (raws if q < 2 else gathered)[k].at[pl.ds(start, stop - start)]
 
-    stages = (0, 0, 1, 1, 2, 2)
+    stages = [None, (0, 0, 1, 1, 2, 7), (0, 0, 1, 1, 7, 2)]
     last_stages = (0, 0, 1, 1, 2, 3, 2, 3)
     sizes = [raw + 1, first, late]
 
     def own_copy(k, g):
         q, r = groups[g]
-        return remote(chunk(raw_m, mine, 0, q, r), chunk(raw_m, mine, k, q, r), s_sem.at[0], b_recv.at[stages[g]], near[k])
+        return remote(chunk(raw_m, mine, 0, q, r), chunk(raw_m, mine, k, q, r), s_sem.at[0], b_recv.at[stages[k][g]], near[k])
 
     def relay_copy(k, q):
         return remote(chunk(raw_m, mine, k, q, q), chunk(raw_m, mine, 3, q, q), s_sem.at[0],
@@ -298,14 +298,16 @@
         for b in range(0, col_blocks, 2):
             stage[k, :, b * TILE:(b + 2) * TILE] = product([mine_k, theirs_k], b).astype(bf16)
 
+    def relay(level):
+        for q in (0, 1, 2, 3, 4, 6, 5, 7):
+            if min(last_stages[q], 2) == level:
+                relay_copy(1 if q in low else 2, q).start()
+
     def arrive(level):
         drain(b_recv.at[level], 2 * sizes[level])
+        relay(level)
         for k in (1, 2):
-            for q in (low if k == 1 else high):
-                if min(last_stages[q], 2) == level:
-                    relay_copy(k, q).start()
-        for k in (1, 2):
-            swap(k, *((0, 1), (2, 3), (4, 7))[level]).start()
+            swap(k, *((0, 1), (2, 3))[level]).start()
 
     arrive(0)
     arrive(1)
@@ -316,7 +318,16 @@
     mend(2, raw_t, theirs, other)
     drain(d_recv.at[5], CAP + 2 * lam_blocks)
     both(0)
-    arrive(2)
+    drain(b_recv.at[2], late)
+    @pl.when(c == 0)
+    def _():
+        relay(2)
+
+    swap(1, 4, 5).start()
+    swap(2, 6, 7).start()
+    drain(b_recv.at[7], late)
+    swap(1, 6, 7).start()
+    swap(2, 4, 5).start()
     here, there = places(mask, 3), places(other, 3)
     ends = [spans[5][0], spans[7][0]]
     for end in ends:
@@ -344,6 +355,11 @@
     drain(b_recv.at[3], raw + 1)
     swap(3, 0, 1).start()
     drain(d_recv.at[6], 2 * (CAP - raw))
+
+    @pl.when(c == 1)
+    def _():
+        relay(2)
+
     both(1)
     drain(b_recv.at[4], first)
     swap(3, 2, 3).start()
@@ -524,7 +540,7 @@
             pltpu.VMEM((col_blocks, inner, TILE), bf16), pltpu.VMEM((blocks,) + tile, bf16),
         ] + masks + [
             pltpu.VMEM((3,) + tile, bf16), pltpu.VMEM((7 * (CAP + 1) + pairs * rows * half // (TILE * TILE),) + tile, bf16),
-            dma((3,)), dma((3,)), dma((2,)), dma((7,)), dma((9,)), pltpu.SemaphoreType.REGULAR((2,)),
+            dma((3,)), dma((3,)), dma((2,)), dma((8,)), dma((9,)), pltpu.SemaphoreType.REGULAR((2,)),
         ] + held + [pltpu.VMEM((raw + 1,) + tile, bf16)] * (2 * n),
         compiler_params=params,
     )(*args)

time: 26.7 us -> 26.5 us (level); the launches traced: 26.2 us -> 26.3 us
  no operation moved by 1% of the time
where the time goes in v6:
time: 26.5 us; the launch traced here: 26.3 us
  Pallas kernels  26.3 us (99%)
    pallas_call x1, Pallas kernels, body(): pl.pallas_call(grid_kernel, out_shape=held_over, in_specs=[anywhere] * 5,...  24.8 us
    pallas_call x1, Pallas kernels, body(): pl.pallas_call(last_kernel, out_shape=jax.ShapeDtypeStruct((1, pairs, row...  1.44 us

profile of v6, /device:TPU:0, one launch (start us, length us, event | category | flops | bytes accessed | tf_op | source)
XLA Modules:
  0.0 26.3 jit_solution(17916884292630430402)
XLA Ops:
  0.0 24.8 %shard_map.55 = (bf16[3,256,1024]{2,1,0:T(8,128)(2,1)S(1)}, bf16[256,1024]{1,0:T(8,128)(2,1)S(1)}, bf16[256,256]{1,0:T(8,128)(2,1)S(1)}, f32[256,1024]{1,0:T(8,128)S(1)}) custom-call(bf16[2,4,256,512]{3,2,1,0:T(8,128)(2,1)} %lam.1, bf16[1,512,1024]{2,1,0:T(8,128)(2,1)} %x.1, bf16[1,512,128]{2,1,0:T(8,128)(2,1)} %y.1, bf16[128,256]{1,0:T(8,128)(2,1)} %t.1, ...), custom_call_target="tpu_custom_call" | custom-call | tf_op jit(solution)/shard_map/pallas_call | solution.py:533
  24.8 1.4 %shard_map.56 = bf16[1,4,256,1024]{3,2,1,0:T(8,128)(2,1)} custom-call(bf16[3,256,1024]{2,1,0:T(8,128)(2,1)S(1)} %get-tuple-element.9.done, bf16[256,1024]{1,0:T(8,128)(2,1)S(1)} %get-tuple-element.10.dense_t, bf16[256,256]{1,0:T(8,128)(2,1)S(1)} %get-tuple-element.11.lam_last, f32[256,1024]{1,0:T(8,128)S(1)} %get-tuple-element.12.acc), custom_call_target="tpu_custom_call" | custom-call | tf_op jit(solution)/shard_map/pallas_call | solution.py:548

commit v7 on v6

--- a/solution.py
+++ b/solution.py
@@ -66,7 +66,7 @@
 
 
 def grid_kernel(lam, x, y, t, mask_any, stage, dense_t, lam_last, acc, lam_m, lam_t, x_v, y_v, t_v, dressed, mask, other,
-                tail, spare, in_sem, s_sem, t_recv, b_recv, d_recv, ready, *bufs):
+                spare, in_sem, s_sem, t_recv, b_recv, d_recv, ready, *bufs):
     n = 4
     mine, theirs, raw_m, raw_t = bufs[:n], bufs[n:2 * n], bufs[2 * n:3 * n], bufs[3 * n:]
     v, c = lax.axis_index("vir"), lax.axis_index("ka")
@@ -114,7 +114,6 @@
     for k in range(n):
         mine[k][CAP] = zero
         theirs[k][CAP] = zero
-    tail[2] = zero
 
     pl.semaphore_wait(barrier, 1 + row + col)
     for k in (1, 2):
@@ -173,9 +172,8 @@
                       b_recv.at[3 + last_stages[q]], near[3 - k])
 
     def swap(k, q, r):
-        sem = 3 + k // 3 if q < 2 else 6 if k < 3 else 8 if q in (5, 7) else 7
-        target = tail.at[pl.ds(q // 7, 1)] if k == 3 and q in (5, 7) else chunk(raw_t, theirs, k, q, r)
-        return remote(chunk(raw_m, mine, k, q, r), target, s_sem.at[0], d_recv.at[sem], to_core)
+        sem = 3 + k // 3 if q < 2 else 6 + k // 3
+        return remote(chunk(raw_m, mine, k, q, r), chunk(raw_t, theirs, k, q, r), s_sem.at[0], d_recv.at[sem], to_core)
 
     own_swap = remote(mine[0].at[pl.ds(0, CAP)], theirs[0].at[pl.ds(0, CAP)], s_sem.at[0], d_recv.at[5], to_core)
     lam_swap = remote(lam.at[partner], lam_t, s_sem.at[0], d_recv.at[5], to_core)
@@ -329,29 +327,7 @@
     swap(1, 6, 7).start()
     swap(2, 4, 5).start()
     here, there = places(mask, 3), places(other, 3)
-    ends = [spans[5][0], spans[7][0]]
-    for end in ends:
-        theirs[3][end] = zero
-    seats = []
-    for end in ends:
-        seat = jnp.int32(-1)
-        for p, slot in enumerate(there):
-            seat = jnp.where(slot == end, p, seat)
-        seats.append(seat)
-    lam_rows = lam_t[ids[3]]
-    for i, seat in enumerate(seats):
-        rows = lam_rows[:, :TILE]
-        for e in range(1, row_blocks):
-            rows = jnp.where(seat >= e * col_blocks, lam_rows[:, e * TILE:(e + 1) * TILE], rows)
-        lam_last[:, i * TILE:(i + 1) * TILE] = rows
-    there = [jnp.where((slot == ends[0]) | (slot == ends[1]), CAP, slot) for slot in there]
-    picks = []
-    for i, seat in enumerate(seats):
-        for b in range(col_blocks):
-            hit = seat == b
-            for e in range(1, row_blocks):
-                hit = hit | (seat == e * col_blocks + b)
-            picks.append(jnp.where(hit, i, 2))
+    lam_last[...] = lam_t[ids[3]]
     drain(b_recv.at[3], raw + 1)
     swap(3, 0, 1).start()
     drain(d_recv.at[6], 2 * (CAP - raw))
@@ -375,13 +351,10 @@
         swap(3, q, q).start()
     for b in range(0, col_blocks, 2):
         acc[:, b * TILE:(b + 2) * TILE] = product([(lam_m[ids[3]], mine[3], here)], b)
-    drain(d_recv.at[7], CAP - raw - 2)
-    for b in range(0, col_blocks, 2):
-        acc[:, b * TILE:(b + 2) * TILE] += product([(lam_t[ids[3]], theirs[3], there)], b)
-    drain(d_recv.at[8], 2)
-    for i, pick in enumerate(picks):
-        e, b = i // col_blocks, i % col_blocks
-        dense_t[e * TILE:(e + 1) * TILE, b * TILE:(b + 1) * TILE] = tail[pick]
+    drain(d_recv.at[7], CAP - raw)
+    for p, slot in enumerate(there):
+        e, b = p // col_blocks, p % col_blocks
+        dense_t[e * TILE:(e + 1) * TILE, b * TILE:(b + 1) * TILE] = theirs[3][slot]
 
     @pl.when(c == 1)
     def _():
@@ -391,24 +364,19 @@
     drain(s_sem.at[0], 3 * (CAP + 1) + CAP + 3 * (CAP + 1) + lam_blocks)
 
 
-def last_kernel(done, dense_t, lam_last, acc, out, stage, sems):
+def last_kernel(done, dense_t, lam_last, acc, out, stage, sem):
     v = lax.axis_index("vir")
     row, col = v // 2, v % 2
     ids = [v, row * 2 + (1 - col), (1 - row) * 2 + col, 3 - v]
-    count = done.shape[0]
     pieces, rows, width = stage.shape
-    copies = [pltpu.make_async_copy(done.at[k], out.at[0, ids[k]], sems.at[pieces + k]) for k in range(count)]
-    for copy in copies:
-        copy.start()
+    for k in range(done.shape[0]):
+        pltpu.make_async_copy(done.at[k], out.at[0, ids[k]], sem.at[0]).start()
     for i in range(pieces):
         columns = slice(i * width, (i + 1) * width)
         stage[i] = (acc[:, columns] + jnp.dot(
             lam_last[...], dense_t[:, columns], preferred_element_type=jnp.float32)).astype(jnp.bfloat16)
-        copy = pltpu.make_async_copy(stage.at[i], out.at[0, ids[3], :, pl.ds(i * width, width)], sems.at[i])
-        copy.start()
-        copies.append(copy)
-    for copy in copies:
-        copy.wait()
+        pltpu.make_async_copy(stage.at[i], out.at[0, ids[3], :, pl.ds(i * width, width)], sem.at[0]).start()
+    pltpu.make_async_copy(out, out, sem.at[0]).wait()
 
 
 def ring_kernel(n, lam, x, y, t, mask_any, out, lam_m, lam_t, x_v, y_v, t_v, dressed, dense_m, dense_t, acc, mask, other,
@@ -529,7 +497,7 @@
             compiler_params=params,
         )(*args)
     raw = CAP // row_blocks
-    held_over = (pltpu.VMEM((n - 1, rows, full), bf16), pltpu.VMEM((2 * TILE, full), bf16), pltpu.VMEM((rows, 2 * TILE), bf16), total)
+    held_over = (pltpu.VMEM((n - 1, rows, full), bf16), dense, pltpu.VMEM((rows, half), bf16), total)
     handed = pl.pallas_call(
         grid_kernel,
         out_shape=held_over,
@@ -539,8 +507,8 @@
             pltpu.VMEM((blocks,) + tile, bf16), pltpu.VMEM((row_blocks, TILE, inner), bf16),
             pltpu.VMEM((col_blocks, inner, TILE), bf16), pltpu.VMEM((blocks,) + tile, bf16),
         ] + masks + [
-            pltpu.VMEM((3,) + tile, bf16), pltpu.VMEM((7 * (CAP + 1) + pairs * rows * half // (TILE * TILE),) + tile, bf16),
-            dma((3,)), dma((3,)), dma((2,)), dma((8,)), dma((9,)), pltpu.SemaphoreType.REGULAR((2,)),
+            pltpu.VMEM((7 * (CAP + 1) + pairs * rows * half // (TILE * TILE),) + tile, bf16),
+            dma((3,)), dma((3,)), dma((2,)), dma((8,)), dma((8,)), pltpu.SemaphoreType.REGULAR((2,)),
         ] + held + [pltpu.VMEM((raw + 1,) + tile, bf16)] * (2 * n),
         compiler_params=params,
     )(*args)
@@ -550,7 +518,7 @@
         out_shape=jax.ShapeDtypeStruct((1, pairs, rows, full), bf16),
         in_specs=[vmem] * 4,
         out_specs=anywhere,
-        scratch_shapes=[pltpu.VMEM((pieces, rows, full // pieces), bf16), dma((pieces + n - 1,))],
+        scratch_shapes=[pltpu.VMEM((pieces, rows, full // pieces), bf16), dma((1,))],
         compiler_params=pltpu.CompilerParams(vmem_limit_bytes=8 * 1024 * 1024),
     )(*handed)
 

time: 26.5 us -> 26.2 us (0.989)
  Pallas kernels: 26.3 us -> 26 us
where the time goes in v7:
time: 26.2 us; the launch traced here: 26 us
  Pallas kernels  26 us (99%)
    pallas_call x1, Pallas kernels, body(): pl.pallas_call(grid_kernel, out_shape=held_over, in_specs=[anywhere] * 5,...  24.7 us
    pallas_call x1, Pallas kernels, body(): pl.pallas_call(last_kernel, out_shape=jax.ShapeDtypeStruct((1, pairs, row...  1.36 us

profile of v7, /device:TPU:0, one launch (start us, length us, event | category | flops | bytes accessed | tf_op | source)
XLA Modules:
  0.0 26.0 jit_solution(3750784920630876613)
XLA Ops:
  0.0 24.7 %shard_map.55 = (bf16[3,256,1024]{2,1,0:T(8,128)(2,1)S(1)}, bf16[512,1024]{1,0:T(8,128)(2,1)S(1)}, bf16[256,512]{1,0:T(8,128)(2,1)S(1)}, f32[256,1024]{1,0:T(8,128)S(1)}) custom-call(bf16[2,4,256,512]{3,2,1,0:T(8,128)(2,1)} %lam.1, bf16[1,512,1024]{2,1,0:T(8,128)(2,1)} %x.1, bf16[1,512,128]{2,1,0:T(8,128)(2,1)} %y.1, bf16[128,256]{1,0:T(8,128)(2,1)} %t.1, ...), custom_call_target="tpu_custom_call" | custom-call | tf_op jit(solution)/shard_map/pallas_call | solution.py:501
  24.7 1.4 %shard_map.56 = bf16[1,4,256,1024]{3,2,1,0:T(8,128)(2,1)} custom-call(bf16[3,256,1024]{2,1,0:T(8,128)(2,1)S(1)} %get-tuple-element.9.done, bf16[512,1024]{1,0:T(8,128)(2,1)S(1)} %get-tuple-element.10.dense_t, bf16[256,512]{1,0:T(8,128)(2,1)S(1)} %get-tuple-element.11.lam_last, f32[256,1024]{1,0:T(8,128)S(1)} %get-tuple-element.12.acc), custom_call_target="tpu_custom_call" | custom-call | tf_op jit(solution)/shard_map/pallas_call | solution.py:516

commit v8 on v7

--- a/solution.py
+++ b/solution.py
@@ -352,9 +352,9 @@
     for b in range(0, col_blocks, 2):
         acc[:, b * TILE:(b + 2) * TILE] = product([(lam_m[ids[3]], mine[3], here)], b)
     drain(d_recv.at[7], CAP - raw)
-    for p, slot in enumerate(there):
-        e, b = p // col_blocks, p % col_blocks
-        dense_t[e * TILE:(e + 1) * TILE, b * TILE:(b + 1) * TILE] = theirs[3][slot]
+    for b in range(0, col_blocks, 2):
+        for e in range(0, row_blocks, 2):
+            dense_t[e * TILE:(e + 2) * TILE, b * TILE:(b + 2) * TILE] = tile(theirs[3], there, e, b)
 
     @pl.when(c == 1)
     def _():

time: 26.2 us -> 26.1 us (level)
  no operation moved by 1% of the time
where the time goes in v8:
time: 26.1 us; the launch traced here: 25.9 us
  Pallas kernels  25.9 us (99%)
    pallas_call x1, Pallas kernels, body(): pl.pallas_call(grid_kernel, out_shape=held_over, in_specs=[anywhere] * 5,...  24.5 us
    pallas_call x1, Pallas kernels, body(): pl.pallas_call(last_kernel, out_shape=jax.ShapeDtypeStruct((1, pairs, row...  1.36 us

profile of v8, /device:TPU:0, one launch (start us, length us, event | category | flops | bytes accessed | tf_op | source)
XLA Modules:
  0.0 25.9 jit_solution(358176634090791496)
XLA Ops:
  0.0 24.5 %shard_map.55 = (bf16[3,256,1024]{2,1,0:T(8,128)(2,1)S(1)}, bf16[512,1024]{1,0:T(8,128)(2,1)S(1)}, bf16[256,512]{1,0:T(8,128)(2,1)S(1)}, f32[256,1024]{1,0:T(8,128)S(1)}) custom-call(bf16[2,4,256,512]{3,2,1,0:T(8,128)(2,1)} %lam.1, bf16[1,512,1024]{2,1,0:T(8,128)(2,1)} %x.1, bf16[1,512,128]{2,1,0:T(8,128)(2,1)} %y.1, bf16[128,256]{1,0:T(8,128)(2,1)} %t.1, ...), custom_call_target="tpu_custom_call" | custom-call | tf_op jit(solution)/shard_map/pallas_call | solution.py:501
  24.5 1.4 %shard_map.56 = bf16[1,4,256,1024]{3,2,1,0:T(8,128)(2,1)} custom-call(bf16[3,256,1024]{2,1,0:T(8,128)(2,1)S(1)} %get-tuple-element.9.done, bf16[512,1024]{1,0:T(8,128)(2,1)S(1)} %get-tuple-element.10.dense_t, bf16[256,512]{1,0:T(8,128)(2,1)S(1)} %get-tuple-element.11.lam_last, f32[256,1024]{1,0:T(8,128)S(1)} %get-tuple-element.12.acc), custom_call_target="tpu_custom_call" | custom-call | tf_op jit(solution)/shard_map/pallas_call | solution.py:516

commit v9 on v8

--- a/solution.py
+++ b/solution.py
@@ -159,7 +159,7 @@
         start, stop = spans[q][0], spans[r][1]
         return (raws if q < 2 else gathered)[k].at[pl.ds(start, stop - start)]
 
-    stages = [None, (0, 0, 1, 1, 2, 7), (0, 0, 1, 1, 7, 2)]
+    stages = [None, (0, 0, 0, 0, 2, 1), (0, 0, 0, 0, 1, 2)]
     last_stages = (0, 0, 1, 1, 2, 3, 2, 3)
     sizes = [raw + 1, first, late]
 
@@ -302,11 +302,11 @@
                 relay_copy(1 if q in low else 2, q).start()
 
     def arrive(level):
-        drain(b_recv.at[level], 2 * sizes[level])
         relay(level)
         for k in (1, 2):
             swap(k, *((0, 1), (2, 3))[level]).start()
 
+    drain(b_recv.at[0], 2 * (sizes[0] + sizes[1]))
     arrive(0)
     arrive(1)
     mend(1, raw_m, mine, mask)
@@ -323,7 +323,7 @@
 
     swap(1, 4, 5).start()
     swap(2, 6, 7).start()
-    drain(b_recv.at[7], late)
+    drain(b_recv.at[1], late)
     swap(1, 6, 7).start()
     swap(2, 4, 5).start()
     here, there = places(mask, 3), places(other, 3)
@@ -508,7 +508,7 @@
             pltpu.VMEM((col_blocks, inner, TILE), bf16), pltpu.VMEM((blocks,) + tile, bf16),
         ] + masks + [
             pltpu.VMEM((7 * (CAP + 1) + pairs * rows * half // (TILE * TILE),) + tile, bf16),
-            dma((3,)), dma((3,)), dma((2,)), dma((8,)), dma((8,)), pltpu.SemaphoreType.REGULAR((2,)),
+            dma((3,)), dma((3,)), dma((2,)), dma((7,)), dma((8,)), pltpu.SemaphoreType.REGULAR((2,)),
         ] + held + [pltpu.VMEM((raw + 1,) + tile, bf16)] * (2 * n),
         compiler_params=params,
     )(*args)

time: 26.1 us -> 26.1 us (level)
  no operation moved by 1% of the time
where the time goes in v9:
time: 26.1 us; the launch traced here: 25.9 us
  Pallas kernels  25.9 us (99%)
    pallas_call x1, Pallas kernels, body(): pl.pallas_call(grid_kernel, out_shape=held_over, in_specs=[anywhere] * 5,...  24.5 us
    pallas_call x1, Pallas kernels, body(): pl.pallas_call(last_kernel, out_shape=jax.ShapeDtypeStruct((1, pairs, row...  1.36 us

profile of v9, /device:TPU:0, one launch (start us, length us, event | category | flops | bytes accessed | tf_op | source)
XLA Modules:
  0.0 25.9 jit_solution(15437913602373502466)
XLA Ops:
  0.0 24.5 %shard_map.55 = (bf16[3,256,1024]{2,1,0:T(8,128)(2,1)S(1)}, bf16[512,1024]{1,0:T(8,128)(2,1)S(1)}, bf16[256,512]{1,0:T(8,128)(2,1)S(1)}, f32[256,1024]{1,0:T(8,128)S(1)}) custom-call(bf16[2,4,256,512]{3,2,1,0:T(8,128)(2,1)} %lam.1, bf16[1,512,1024]{2,1,0:T(8,128)(2,1)} %x.1, bf16[1,512,128]{2,1,0:T(8,128)(2,1)} %y.1, bf16[128,256]{1,0:T(8,128)(2,1)} %t.1, ...), custom_call_target="tpu_custom_call" | custom-call | tf_op jit(solution)/shard_map/pallas_call | solution.py:501
  24.5 1.4 %shard_map.56 = bf16[1,4,256,1024]{3,2,1,0:T(8,128)(2,1)} custom-call(bf16[3,256,1024]{2,1,0:T(8,128)(2,1)S(1)} %get-tuple-element.9.done, bf16[512,1024]{1,0:T(8,128)(2,1)S(1)} %get-tuple-element.10.dense_t, bf16[256,512]{1,0:T(8,128)(2,1)S(1)} %get-tuple-element.11.lam_last, f32[256,1024]{1,0:T(8,128)S(1)} %get-tuple-element.12.acc), custom_call_target="tpu_custom_call" | custom-call | tf_op jit(solution)/shard_map/pallas_call | solution.py:516

commit v10 on v8

--- a/solution.py
+++ b/solution.py
@@ -329,12 +329,13 @@
     here, there = places(mask, 3), places(other, 3)
     lam_last[...] = lam_t[ids[3]]
     drain(b_recv.at[3], raw + 1)
+
+    @pl.when(c == 1)
+    def _():
+        relay(2)
+
     swap(3, 0, 1).start()
     drain(d_recv.at[6], 2 * (CAP - raw))
-
-    @pl.when(c == 1)
-    def _():
-        relay(2)
 
     both(1)
     drain(b_recv.at[4], first)

time: 26.1 us -> 26.1 us (level)
  no operation moved by 1% of the time
where the time goes in v10:
time: 26.1 us; the launch traced here: 25.9 us
  Pallas kernels  25.9 us (99%)
    pallas_call x1, Pallas kernels, body(): pl.pallas_call(grid_kernel, out_shape=held_over, in_specs=[anywhere] * 5,...  24.5 us
    pallas_call x1, Pallas kernels, body(): pl.pallas_call(last_kernel, out_shape=jax.ShapeDtypeStruct((1, pairs, row...  1.36 us

profile of v10, /device:TPU:0, one launch (start us, length us, event | category | flops | bytes accessed | tf_op | source)
XLA Modules:
  0.0 25.9 jit_solution(13400992014836309538)
XLA Ops:
  0.0 24.5 %shard_map.55 = (bf16[3,256,1024]{2,1,0:T(8,128)(2,1)S(1)}, bf16[512,1024]{1,0:T(8,128)(2,1)S(1)}, bf16[256,512]{1,0:T(8,128)(2,1)S(1)}, f32[256,1024]{1,0:T(8,128)S(1)}) custom-call(bf16[2,4,256,512]{3,2,1,0:T(8,128)(2,1)} %lam.1, bf16[1,512,1024]{2,1,0:T(8,128)(2,1)} %x.1, bf16[1,512,128]{2,1,0:T(8,128)(2,1)} %y.1, bf16[128,256]{1,0:T(8,128)(2,1)} %t.1, ...), custom_call_target="tpu_custom_call" | custom-call | tf_op jit(solution)/shard_map/pallas_call | solution.py:502
  24.5 1.4 %shard_map.56 = bf16[1,4,256,1024]{3,2,1,0:T(8,128)(2,1)} custom-call(bf16[3,256,1024]{2,1,0:T(8,128)(2,1)S(1)} %get-tuple-element.9.done, bf16[512,1024]{1,0:T(8,128)(2,1)S(1)} %get-tuple-element.10.dense_t, bf16[256,512]{1,0:T(8,128)(2,1)S(1)} %get-tuple-element.11.lam_last, f32[256,1024]{1,0:T(8,128)S(1)} %get-tuple-element.12.acc), custom_call_target="tpu_custom_call" | custom-call | tf_op jit(solution)/shard_map/pallas_call | solution.py:517
